TPU v7x, 256 devices: a whole 4x4x8 slice. The times are simulated.
256 devices in a mesh: dp: 8 (over x_lo, y), mp: 32 (over z, x_hi, core).
Axes of the slice: x: 4 (x_hi: 2, x_lo: 2; x = x_hi * 2 + x_lo), y: 4, z: 8, core: 2. Of those that a mesh axis runs over, the one named last changes fastest.
Arguments:
- tokens: bfloat16 [1024, 6144], P(('dp', 'mp')), may hold values from -6 to 6
- norm_gain: float32 [6144], replicated, may hold values from 0.5 to 1.5
- w_query: bfloat16 [6144, 4096], P('dp', 'mp'), as said below
- w_key: bfloat16 [6144, 4096], P('dp', 'mp'), as said below
- w_value: bfloat16 [6144, 4096], P('dp', 'mp'), may hold values from -0.078125 to 0.078125
- w_inner: bfloat16 [6144, 24576], P('dp', 'mp'), may hold values from -0.078125 to 0.078125
- bias_inner: float32 [24576], P('mp'), may hold values from -3 to 3
- w_attn_out: bfloat16 [4096, 6144], P('mp', 'dp'), may hold values from -0.09375 to 0.09375
- w_outer: bfloat16 [24576, 6144], P('mp', 'dp'), may hold values from -0.0390625 to 0.0390625
- temper: float32 [32], P('mp'), may hold values from 0.5 to 24
Outputs:
- result: bfloat16 [1024, 6144], P(('dp', 'mp'))
Inputs may be any that keep to these rules, and one draw needn't show every extreme that they name: `w_query`: entries of order 6144 ** -0.5. `w_key`: entries of order 6144 ** -0.5.
All inputs are finite; a program needn't handle non-finite values.
Results may differ from a plain program's by a relative error of at most 0.023.
Values may be sent and summed in bfloat16 or wider, within the bound.
No kernel may reach another device: no remote copies, remote signals or barrier semaphores. Data moves between devices by JAX's collectives and lax.ppermute only.
A program may use at most 64 MiB of HBM per device.

v0:
```python
import math

import jax
import jax.numpy as jnp
from jax import lax
from jax.sharding import Mesh
from jax.sharding import PartitionSpec as P


HEAD = 128
DP = ("xl", "y")
MP = ("z", "xh", "c")
ALL = DP + MP
BF = jnp.bfloat16
F32 = jnp.float32


def normalize(values):
    center = values - jnp.mean(values, axis=-1, keepdims=True)
    spread = jnp.mean(center * center, axis=-1, keepdims=True)
    return center * lax.rsqrt(spread + 1e-06)


def partner(array, axis):
    return lax.ppermute(array, axis, [(0, 1), (1, 0)])


def exchange(pieces, axes):
    return lax.all_to_all(pieces, axes, split_axis=0, concat_axis=0, tiled=True)


def dot(a, b):
    return lax.dot_general(a, b, (((a.ndim - 1,), (0,)), ((), ())), preferred_element_type=F32)


def own_first(array, dim):
    flipped = jnp.flip(array, dim)
    return jnp.where(lax.axis_index("xl") == 0, array, flipped)


def block(
    tokens, norm_gain, w_query, w_key, w_value, w_inner, bias_inner, w_attn_out, w_outer, temper
):
    count, width = tokens.shape
    n_xl, n_y, n_z, n_xh = (lax.axis_size(a) for a in ("xl", "y", "z", "xh"))
    cols = width // (n_xl * n_y)
    local = tokens.astype(F32)
    normed = (normalize(local) * norm_gain).astype(BF)
    beside = partner(normed, "xh")
    first = lax.axis_index("xh") == 0
    rows = jnp.concatenate(
        (jnp.where(first, normed, beside), jnp.where(first, beside, normed)), axis=0
    )
    w_qkv = jnp.concatenate((w_query, w_key, w_value), axis=1)
    w_out = jnp.concatenate((w_attn_out, w_outer), axis=0)
    w_qkv_p = partner(w_qkv, "xl")
    w_inner_p = partner(w_inner, "xl")
    w_out_p = partner(w_out, "xl")
    split = own_first(rows.reshape(n_xh * count, n_xl, n_y, cols), 1)
    split = split.transpose(2, 0, 1, 3)
    pieces = jnp.broadcast_to(
        split[:, None], (n_y, n_z, n_xh * count, n_xl, cols)
    ).reshape(n_y * n_z, n_xh * count, n_xl * cols)
    mine = exchange(pieces, ("y", "z"))
    mine = mine.reshape(n_y, -1, n_xl * cols)
    theirs = partner(mine, "c")
    image = jnp.concatenate((mine, theirs), axis=1)
    patches = image.shape[1]

    def projected(weights, weights_p):
        partial = dot(image[..., :cols], weights) + dot(image[..., cols:], weights_p)
        arrived = exchange(partial.astype(BF), "y")
        return arrived.astype(F32).sum(axis=0)

    qkv = projected(w_qkv, w_qkv_p)
    query_norm = normalize(qkv[:, :HEAD].astype(BF).astype(F32)).astype(BF)
    key_norm = normalize(qkv[:, HEAD : 2 * HEAD].astype(BF).astype(F32)).astype(BF)
    value = qkv[:, 2 * HEAD :].astype(BF)
    scores = jnp.einsum("qc,kc->qk", query_norm, key_norm, preferred_element_type=F32)
    scores = scores * (temper / math.sqrt(HEAD))
    probs = jax.nn.softmax(scores, axis=-1).astype(BF)
    mixed = dot(probs, value).astype(BF)
    inner = projected(w_inner, w_inner_p) + bias_inner
    activ = jax.nn.gelu(inner, approximate=False).astype(BF)
    features = jnp.concatenate((mixed, activ), axis=1)
    features = exchange(jnp.broadcast_to(features, (n_y, *features.shape)), "y")
    half = patches // 2

    def output(part):
        return jnp.concatenate((dot(part, w_out), dot(part, w_out_p)), axis=-1)

    sent = output(features[:, half:]).astype(BF)
    summed = (output(features[:, :half]) + partner(sent, "c").astype(F32)).astype(BF)
    pieces = summed.reshape(n_y * n_z * n_xh, count, n_xl * cols)
    arrived = exchange(pieces, ("y", "z", "xh"))
    total = arrived.reshape(n_y, n_z * n_xh, count, n_xl, cols).astype(F32).sum(axis=1)
    total = own_first(total.transpose(1, 2, 0, 3), 1).reshape(count, width)
    return (local + total).astype(BF)


def solution(mesh):
    finer = Mesh(mesh.devices.reshape(2, 4, 8, 2, 2), ALL)
    return jax.shard_map(
        block,
        mesh=finer,
        in_specs=(
            P(ALL, None),
            P(),
            P(DP, MP),
            P(DP, MP),
            P(DP, MP),
            P(DP, MP),
            P(MP),
            P(MP, DP),
            P(MP, DP),
            P(MP),
        ),
        out_specs=P(ALL, None),
        check_vma=False,
    )
```

profile of v0, /device:TPU:8, one launch (start us, length us, event | category | flops | bytes accessed | tf_op | source)
XLA Modules:
  0.0 149.5 jit_solution(6755798080559915301)
XLA Ops:
  0.0 1.0 convert_reduce_fusion.1
  1.0 1.0 fusion.39
  2.0 0.9 fusion.41
  2.9 3.1 %collective-permute-start = (bf16[4,6144]{1,0:T(4,128)(2,1)S(1)}, bf16[4,6144]{1,0:T(4,128)(2,1)S(1)}, u32[]{:S(2)}, u32[]{:S(2)}) collective-permute-start(bf16[4,6144]{1,0:T(4,128)(2,1)S(1)} %fusion.41), channel_id=1, source_target_pairs={{0,2},{2,0},{1,3},{3,1},{4,6},{6,4},{5,7},{7,5},{8,10},{10,8},{9,1... | collective-permute-start | bytes 147464 | tf_op jit(solution)/shard_map/ppermute | solution.py:25
  6.0 2.6 %collective-permute-done = bf16[4,6144]{1,0:T(4,128)(2,1)S(1)} collective-permute-done((bf16[4,6144]{1,0:T(4,128)(2,1)S(1)}, bf16[4,6144]{1,0:T(4,128)(2,1)S(1)}, u32[]{:S(2)}, u32[]{:S(2)}) %collective-permute-start) | collective-permute-done | bytes 49184 | tf_op jit(solution)/shard_map/ppermute | solution.py:25
  8.6 0.9 broadcast_select_fusion.2
  9.7 0.9 broadcast_in_dim.4
  10.6 11.8 %all-to-all-start = ((bf16[32,8,1536]{2,1,0:T(8,128)(2,1)}), bf16[32,8,1536]{2,1,0:T(8,128)(2,1)S(1)}, u32[]{:S(2)}, u32[]{:S(2)}) async-start(bf16[32,8,1536]{2,1,0:T(8,128)(2,1)} %bitcast.2), calls=%async_computation | async-start | bytes 1572864 | tf_op jit(solution)/shard_map/all_to_all | solution.py:29
  22.5 1.6 %collective-permute-start.3 = (bf16[768,768]{1,0:T(8,128)(2,1)}, bf16[768,768]{1,0:T(8,128)(2,1)}, u32[]{:S(2)}, u32[]{:S(2)}) collective-permute-start(bf16[768,768]{1,0:T(8,128)(2,1)} %param.15), channel_id=1, source_target_pairs={{0,128},{128,0},{1,129},{129,1},{2,130},{130,2},{3,131},{131,3},{4... | collective-permute-start | bytes 3538952 | tf_op jit(solution)/shard_map/ppermute | solution.py:25
  24.1 0.7 constant_dynamic-update-slice_fusion.2
  24.8 17.1 %all-to-all-done = bf16[32,8,1536]{2,1,0:T(8,128)(2,1)S(1)} async-done(((bf16[32,8,1536]{2,1,0:T(8,128)(2,1)}), bf16[32,8,1536]{2,1,0:T(8,128)(2,1)S(1)}, u32[]{:S(2)}, u32[]{:S(2)}) %all-to-all-start) | async-done | bytes 786464 | tf_op jit(solution)/shard_map/all_to_all | solution.py:29
  41.8 0.7 constant_dynamic-update-slice_fusion.1
  42.6 0.7 constant_dynamic-update-slice_fusion
  43.3 1.5 collective-permute-start.2
  44.8 1.3 constant_dynamic-update-slice_fusion.3
  46.1 0.6 collective-permute-start.4
  47.4 16.2 %collective-permute-done.2 = bf16[768,384]{1,0:T(8,128)(2,1)S(1)} collective-permute-done((bf16[768,384]{1,0:T(8,128)(2,1)}, bf16[768,384]{1,0:T(8,128)(2,1)S(1)}, u32[]{:S(2)}, u32[]{:S(2)}) %collective-permute-start.2) | collective-permute-done | bytes 589856 | tf_op jit(solution)/shard_map/ppermute | solution.py:25
  63.6 0.6 fusion.20
  64.2 2.4 %fusion.9 = bf16[4,128,384]{2,1,0:T(8,128)(2,1)} fusion(f32[4,128,384]{2,1,0:T(8,128)S(1)} %fusion.20, bf16[768,384]{1,0:T(8,128)(2,1)} %constant_dynamic-update-slice_fusion, bf16[4,64,1536]{2,1,0:T(8,128)(2,1)S(1)} %bitcast.36, bf16[4,64,1536]{2,1,0:T(8,128)(2,1)S(1)} %collective-permute-done.1), kind=kOutput, calls=%fused_computation.15 | convolution fusion | flops 303955968 | bytes 3342336 | tf_op jit(solution)/shard_map/dot_general | solution.py:33
  66.6 4.8 %all-to-all-start.1 = ((bf16[4,128,384]{2,1,0:T(8,128)(2,1)}), bf16[4,128,384]{2,1,0:T(8,128)(2,1)S(1)}, u32[]{:S(2)}, u32[]{:S(2)}) async-start(bf16[4,128,384]{2,1,0:T(8,128)(2,1)} %fusion.9), calls=%async_computation.1 | async-start | bytes 786432 | tf_op jit(solution)/shard_map/all_to_all | solution.py:29
  71.4 2.1 %fusion.16 = f32[4,128,768]{2,1,0:T(8,128)S(1)} fusion(bf16[768,768]{1,0:T(8,128)(2,1)} %collective-permute-done.3, bf16[4,64,1536]{2,1,0:T(8,128)(2,1)S(1)} %collective-permute-done.1, bf16[4,64,1536]{2,1,0:T(8,128)(2,1)S(1)} %bitcast.37), kind=kOutput, calls=%fused_computation.18 | convolution fusion | flops 605552640 | bytes 4325376 | tf_op jit(solution)/shard_map/dot_general | solution.py:33
  73.5 3.0 %add_convert_fusion = bf16[4,128,768]{2,1,0:T(8,128)(2,1)} fusion(f32[4,128,768]{2,1,0:T(8,128)S(1)} %fusion.16, bf16[768,768]{1,0:T(8,128)(2,1)} %param.15, bf16[4,64,1536]{2,1,0:T(8,128)(2,1)S(1)} %bitcast.38, bf16[4,64,1536]{2,1,0:T(8,128)(2,1)S(1)} %collective-permute-done.1), kind=kOutput, calls=%fused_computation.5 | convolution fusion | flops 606339072 | bytes 5111808 | tf_op jit(solution)/shard_map/dot_general | solution.py:33
  76.4 0.9 all-to-all-done.1
  77.3 4.9 %all-to-all-start.2 = ((bf16[4,128,768]{2,1,0:T(8,128)(2,1)}), bf16[4,128,768]{2,1,0:T(8,128)(2,1)S(1)}, u32[]{:S(2)}, u32[]{:S(2)}) async-start(bf16[4,128,768]{2,1,0:T(8,128)(2,1)} %add_convert_fusion), calls=%async_computation.2 | async-start | bytes 1572864 | tf_op jit(solution)/shard_map/all_to_all | solution.py:29
  82.3 0.1 reduce
  82.3 0.1 convert_reduce_fusion.3
  82.4 0.2 fusion.50
  82.6 0.3 fusion.68
  83.0 0.2 convolution_convert_fusion
  83.2 0.1 copy.19
  83.3 7.0 %all-to-all-done.2 = bf16[4,128,768]{2,1,0:T(8,128)(2,1)S(1)} async-done(((bf16[4,128,768]{2,1,0:T(8,128)(2,1)}), bf16[4,128,768]{2,1,0:T(8,128)(2,1)S(1)}, u32[]{:S(2)}, u32[]{:S(2)}) %all-to-all-start.2) | async-done | bytes 786464 | tf_op jit(solution)/shard_map/all_to_all | solution.py:29
  90.3 0.1 convert_reduce_fusion
  90.4 0.9 fusion.29
  91.3 0.1 broadcast_in_dim.5
  91.4 12.6 %all_to_all.25 = bf16[4,128,896]{2,1,0:T(8,128)(2,1)S(1)} all-to-all(bf16[4,128,896]{2,1,0:T(8,128)(2,1)S(1)} %broadcast_in_dim.5), channel_id=1, replica_groups=mesh['xl'=2,'y'=4,'z'=8,'xh'=2,'c'=2] {'y'}, dimensions={0} | all-to-all | bytes 1835008 | tf_op jit(solution)/shard_map/all_to_all | solution.py:29
  104.0 0.6 fusion.10
  104.6 1.9 %fusion.13 = bf16[4,64,768]{2,1,0:T(8,128)(2,1)S(1)} fusion(bf16[896,768]{1,0:T(8,128)(2,1)} %collective-permute-done.4, bf16[4,128,896]{2,1,0:T(8,128)(2,1)S(1)} %all_to_all.25), kind=kOutput, calls=%fused_computation.17 | convolution fusion | flops 352518144 | bytes 2228224 | tf_op jit(solution)/shard_map/dot_general | solution.py:33
  106.6 0.1 collective-permute-start.5
  106.7 0.6 fusion.7
  107.2 1.9 %fusion.3 = f32[4,64,768]{2,1,0:T(8,128)S(1)} fusion(bf16[896,768]{1,0:T(8,128)(2,1)} %collective-permute-done.4, bf16[4,128,896]{2,1,0:T(8,128)(2,1)S(1)} %all_to_all.25), kind=kOutput, calls=%fused_computation.8 | convolution fusion | flops 352321536 | bytes 2621440 | tf_op jit(solution)/shard_map/dot_general | solution.py:33
  109.2 0.2 fusion
  109.3 0.2 reshape.63
  109.5 37.2 %all_to_all.26 = bf16[64,4,1536]{2,1,0:T(4,128)(2,1)S(1)} all-to-all(bf16[64,4,1536]{2,1,0:T(4,128)(2,1)S(1)} %reshape.63), channel_id=1, replica_groups=mesh['xl'=2,'y'=4,'z'=8,'xh'=2,'c'=2] {'y','z','xh'}, dimensions={0} | all-to-all | bytes 1572864 | tf_op jit(solution)/shard_map/all_to_all | solution.py:29
  146.7 1.0 reshape.65
  147.7 0.5 reduce_sum.99
  148.3 0.4 rev.9
  148.8 0.1 reshape.64
  148.8 0.6 fusion.42
  (31 shorter events, 0.4 us)
Async XLA Ops:
  2.9 5.7 %collective-permute-start = (bf16[4,6144]{1,0:T(4,128)(2,1)S(1)}, bf16[4,6144]{1,0:T(4,128)(2,1)S(1)}, u32[]{:S(2)}, u32[]{:S(2)}) collective-permute-start(bf16[4,6144]{1,0:T(4,128)(2,1)S(1)} %fusion.41), channel_id=1, source_target_pairs={{0,2},{2,0},{1,3},{3,1},{4,6},{6,4},{5,7},{7,5},{8,10},{10,8},{9,1... | collective-permute-start | bytes 147464 | tf_op jit(solution)/shard_map/ppermute | solution.py:25
  9.6 14.5 %copy-start.1 = (bf16[768,128]{1,0:T(8,128)(2,1)S(1)}, bf16[768,128]{1,0:T(8,128)(2,1)}, u32[]{:S(2)}) copy-start(bf16[768,128]{1,0:T(8,128)(2,1)} %param.12) | copy-start | bytes 589828
  9.7 32.2 %copy-start.2 = (bf16[768,128]{1,0:T(8,128)(2,1)S(1)}, bf16[768,128]{1,0:T(8,128)(2,1)}, u32[]{:S(2)}) copy-start(bf16[768,128]{1,0:T(8,128)(2,1)} %param.13) | copy-start | bytes 589828
  9.7 32.9 %copy-start.3 = (bf16[768,128]{1,0:T(8,128)(2,1)S(1)}, bf16[768,128]{1,0:T(8,128)(2,1)}, u32[]{:S(2)}) copy-start(bf16[768,128]{1,0:T(8,128)(2,1)} %param.14) | copy-start | bytes 589828
  10.6 34.1 %copy-start.4 = (bf16[128,768]{1,0:T(8,128)(2,1)S(1)}, bf16[128,768]{1,0:T(8,128)(2,1)}, u32[]{:S(2)}) copy-start(bf16[128,768]{1,0:T(8,128)(2,1)} %param.17) | copy-start | bytes 589828
  10.6 31.2 %all-to-all-start = ((bf16[32,8,1536]{2,1,0:T(8,128)(2,1)}), bf16[32,8,1536]{2,1,0:T(8,128)(2,1)S(1)}, u32[]{:S(2)}, u32[]{:S(2)}) async-start(bf16[32,8,1536]{2,1,0:T(8,128)(2,1)} %bitcast.2), calls=%async_computation | async-start | bytes 1572864 | tf_op jit(solution)/shard_map/all_to_all | solution.py:29
  22.5 48.9 %collective-permute-start.3 = (bf16[768,768]{1,0:T(8,128)(2,1)}, bf16[768,768]{1,0:T(8,128)(2,1)}, u32[]{:S(2)}, u32[]{:S(2)}) collective-permute-start(bf16[768,768]{1,0:T(8,128)(2,1)} %param.15), channel_id=1, source_target_pairs={{0,128},{128,0},{1,129},{129,1},{2,130},{130,2},{3,131},{131,3},{4... | collective-permute-start | bytes 3538952 | tf_op jit(solution)/shard_map/ppermute | solution.py:25
  41.8 21.8 %collective-permute-start.1 = (bf16[4,64,1536]{2,1,0:T(8,128)(2,1)S(1)}, bf16[4,64,1536]{2,1,0:T(8,128)(2,1)S(1)}, u32[]{:S(2)}, u32[]{:S(2)}) collective-permute-start(bf16[4,64,1536]{2,1,0:T(8,128)(2,1)S(1)} %bitcast.34), channel_id=1, source_target_pairs={{0,1},{1,0},{2,3},{3,2},{4,5},{5,4},{6,7},{7,6},{8,9},{9,8},{10,11... | collective-permute-start | bytes 2359304 | tf_op jit(solution)/shard_map/ppermute | solution.py:25
  43.3 20.3 %collective-permute-start.2 = (bf16[768,384]{1,0:T(8,128)(2,1)}, bf16[768,384]{1,0:T(8,128)(2,1)S(1)}, u32[]{:S(2)}, u32[]{:S(2)}) collective-permute-start(bf16[768,384]{1,0:T(8,128)(2,1)} %constant_dynamic-update-slice_fusion), channel_id=1, source_target_pairs={{0,128},{128,0},{1,129},{129,1},{2,130},{130,2},{3,131},{131,3},{4... | collective-permute-start | bytes 1769480 | tf_op jit(solution)/shard_map/ppermute | solution.py:25
  46.1 58.4 %collective-permute-start.4 = (bf16[896,768]{1,0:T(8,128)(2,1)S(1)}, bf16[896,768]{1,0:T(8,128)(2,1)}, u32[]{:S(2)}, u32[]{:S(2)}) collective-permute-start(bf16[896,768]{1,0:T(8,128)(2,1)S(1)} %constant_dynamic-update-slice_fusion.3), channel_id=1, source_target_pairs={{0,128},{128,0},{1,129},{129,1},{2,130},{130,2},{3,131},{131,3},{4... | collective-permute-start | bytes 4128776 | tf_op jit(solution)/shard_map/ppermute | solution.py:25
  66.6 10.8 %all-to-all-start.1 = ((bf16[4,128,384]{2,1,0:T(8,128)(2,1)}), bf16[4,128,384]{2,1,0:T(8,128)(2,1)S(1)}, u32[]{:S(2)}, u32[]{:S(2)}) async-start(bf16[4,128,384]{2,1,0:T(8,128)(2,1)} %fusion.9), calls=%async_computation.1 | async-start | bytes 786432 | tf_op jit(solution)/shard_map/all_to_all | solution.py:29
  77.3 13.0 %all-to-all-start.2 = ((bf16[4,128,768]{2,1,0:T(8,128)(2,1)}), bf16[4,128,768]{2,1,0:T(8,128)(2,1)S(1)}, u32[]{:S(2)}, u32[]{:S(2)}) async-start(bf16[4,128,768]{2,1,0:T(8,128)(2,1)} %add_convert_fusion), calls=%async_computation.2 | async-start | bytes 1572864 | tf_op jit(solution)/shard_map/all_to_all | solution.py:29
  82.3 8.1 %copy-start.5 = (f32[768]{0:T(1024)S(1)}, f32[768]{0:T(1024)}, u32[]{:S(2)}) copy-start(f32[768]{0:T(1024)} %param.16) | copy-start | bytes 9220
  106.6 2.6 %collective-permute-start.5 = (bf16[4,64,1536]{2,1,0:T(8,128)(2,1)S(1)}, bf16[4,64,1536]{2,1,0:T(8,128)(2,1)S(1)}, u32[]{:S(2)}, u32[]{:S(2)}) collective-permute-start(bf16[4,64,1536]{2,1,0:T(8,128)(2,1)S(1)} %pad_maximum_fusion.1), channel_id=1, source_target_pairs={{0,1},{1,0},{2,3},{3,2},{4,5},{5,4},{6,7},{7,6},{8,9},{9,8},{10,11... | collective-permute-start | bytes 2359304 | tf_op jit(solution)/shard_map/ppermute | solution.py:25
  147.7 1.1 copy-start
where the time goes:
time: 151 us; the launch traced here: 149 us
  blocking collectives  49.8 us (33%)
  waiting for transfers between devices  43.7 us (29%)
  starting transfers between devices  28.5 us (19%)
  matrix products  13.4 us (9%)
  other arithmetic  6.79 us (4%)
  local copies, waits for them, and re-layouts  6.29 us (4%)
    all_to_all x2, blocking collectives, exchange(): return lax.all_to_all(pieces, axes, split_axis=0, concat_axis=0, tiled=True)  49.8 us
    all_to_all x3, waiting for transfers between devices, exchange(): return lax.all_to_all(pieces, axes, split_axis=0, concat_axis=0, tiled=True)  24.9 us
    all_to_all x3, starting transfers between devices, exchange(): return lax.all_to_all(pieces, axes, split_axis=0, concat_axis=0, tiled=True)  21.6 us
    ppermute x6, waiting for transfers between devices, partner(): return lax.ppermute(array, axis, [(0, 1), (1, 0)])  18.8 us
    dot_general x9, matrix products, dot(): lax.dot_general(a, b, (((a.ndim - 1,), (0,)), ((), ())), preferred_elemen...  13.2 us
    ppermute x6, starting transfers between devices, partner(): return lax.ppermute(array, axis, [(0, 1), (1, 0)])  6.9 us
  transfers between devices with their start and end apart: 9, of which 5 were waited for; matrix products, arithmetic and copies ran while one was open for 11% of the time, Pallas kernels for 0%

commit v1 on v0

--- a/solution.py
+++ b/solution.py
@@ -3,6 +3,8 @@
 import jax
 import jax.numpy as jnp
 from jax import lax
+from jax.experimental import pallas as pl
+from jax.experimental.pallas import tpu as pltpu
 from jax.sharding import Mesh
 from jax.sharding import PartitionSpec as P
 
@@ -38,6 +40,58 @@
     return jnp.where(lax.axis_index("xl") == 0, array, flipped)
 
 
+def project_kernel(mine, theirs, *refs):
+    sources = refs[:4]
+    out = refs[4]
+    tokens, kept, sems = refs[5:7], refs[7:11], refs[11]
+    copies = [
+        pltpu.make_async_copy(src, dst, sems.at[n])
+        for n, (src, dst) in enumerate(zip((mine, theirs, *sources), (*tokens, *kept)))
+    ]
+    for copy in (copies[0], copies[2], copies[3], copies[1], copies[4], copies[5]):
+        copy.start()
+    images, half, width = tokens[0].shape
+    cols = width // 2
+    for n in (0, 2, 3):
+        copies[n].wait()
+    for part in range(2):
+        if part:
+            copies[1].wait()
+        rows = tokens[part][...].reshape(images * half, width)
+        for n in range(3):
+            if not part and n == 1:
+                for m in (4, 5):
+                    copies[m].wait()
+            w, w_p = kept[:2] if n == 0 else kept[2:]
+            at = slice(0, 384) if n == 0 else slice((n - 1) * 384, n * 384)
+            value = dot(rows[:, :cols], w[:, at]) + dot(rows[:, cols:], w_p[:, at])
+            out[:, part * half : (part + 1) * half, n * 384 : (n + 1) * 384] = value.astype(
+                BF
+            ).reshape(images, half, 384)
+
+
+def project(mine, theirs, *weights):
+    images, half, width = mine.shape
+    columns = weights[0].shape[1] + weights[2].shape[1]
+    spec = pl.BlockSpec(memory_space=pl.ANY)
+    return pl.pallas_call(
+        project_kernel,
+        out_shape=jax.ShapeDtypeStruct((images, 2 * half, columns), BF),
+        in_specs=[spec] * 6,
+        out_specs=pl.BlockSpec(memory_space=pltpu.VMEM),
+        scratch_shapes=[pltpu.VMEM(mine.shape, BF)] * 2
+        + [pltpu.VMEM(w.shape, BF) for w in weights]
+        + [pltpu.SemaphoreType.DMA((6,))],
+        compiler_params=pltpu.CompilerParams(vmem_limit_bytes=24 * 1024 * 1024),
+        cost_estimate=pl.CostEstimate(
+            flops=4 * images * half * width * columns,
+            bytes_accessed=7 * 1024 * 1024,
+            transcendentals=0,
+        ),
+        name="project",
+    )(mine, theirs, *weights)
+
+
 def block(
     tokens, norm_gain, w_query, w_key, w_value, w_inner, bias_inner, w_attn_out, w_outer, temper
 ):
@@ -64,23 +118,18 @@
     mine = exchange(pieces, ("y", "z"))
     mine = mine.reshape(n_y, -1, n_xl * cols)
     theirs = partner(mine, "c")
-    image = jnp.concatenate((mine, theirs), axis=1)
-    patches = image.shape[1]
-
-    def projected(weights, weights_p):
-        partial = dot(image[..., :cols], weights) + dot(image[..., cols:], weights_p)
-        arrived = exchange(partial.astype(BF), "y")
-        return arrived.astype(F32).sum(axis=0)
-
-    qkv = projected(w_qkv, w_qkv_p)
-    query_norm = normalize(qkv[:, :HEAD].astype(BF).astype(F32)).astype(BF)
-    key_norm = normalize(qkv[:, HEAD : 2 * HEAD].astype(BF).astype(F32)).astype(BF)
-    value = qkv[:, 2 * HEAD :].astype(BF)
+    patches = 2 * mine.shape[1]
+    partial = project(mine, theirs, w_qkv, w_qkv_p, w_inner, w_inner_p)
+    sums = exchange(partial, "y").astype(F32).sum(axis=0)
+    scale = temper / math.sqrt(HEAD)
+    query_norm = normalize(sums[:, :HEAD].astype(BF).astype(F32)).astype(BF)
+    key_norm = normalize(sums[:, HEAD : 2 * HEAD].astype(BF).astype(F32)).astype(BF)
+    value = sums[:, 2 * HEAD : 3 * HEAD].astype(BF)
     scores = jnp.einsum("qc,kc->qk", query_norm, key_norm, preferred_element_type=F32)
-    scores = scores * (temper / math.sqrt(HEAD))
+    scores = scores * scale
     probs = jax.nn.softmax(scores, axis=-1).astype(BF)
     mixed = dot(probs, value).astype(BF)
-    inner = projected(w_inner, w_inner_p) + bias_inner
+    inner = sums[:, 3 * HEAD :] + bias_inner
     activ = jax.nn.gelu(inner, approximate=False).astype(BF)
     features = jnp.concatenate((mixed, activ), axis=1)
     features = exchange(jnp.broadcast_to(features, (n_y, *features.shape)), "y")

time: 151 us -> 148 us (0.980)
  matrix products: 13.4 us -> 5.44 us
  waiting for transfers between devices: 43.7 us -> 49.3 us
  Pallas kernels: 0 us -> 5.32 us
  starting transfers between devices: 28.5 us -> 24.7 us
  local copies, waits for them, and re-layouts: 6.29 us -> 4.35 us
    dot_general x9 -> x5, matrix products: 13.2 us -> 5.17 us  [dot(): lax.dot_general(a, b, (((a.ndim - 1,), (0,)), ((), ())), preferred_elemen...]
    pallas_call x0 -> x1, Pallas kernels: none -> 5.32 us  [project(): pl.pallas_call(project_kernel, out_shape=jax.ShapeDtypeStruct((images, 2...]
    all_to_all x3 -> x2, starting transfers between devices: 21.6 us -> 16.8 us  [exchange(): return lax.all_to_all(pieces, axes, split_axis=0, concat_axis=0, tiled=True)]
    all_to_all x3 -> x2, waiting for transfers between devices: 24.9 us -> 27.8 us  [exchange(): return lax.all_to_all(pieces, axes, split_axis=0, concat_axis=0, tiled=True)]
    ppermute x6, waiting for transfers between devices: 18.8 us -> 21.5 us  [partner(): return lax.ppermute(array, axis, [(0, 1), (1, 0)])]
  transfers between devices with their start and end apart: 9 -> 8, of which waited for: 5 -> 5; matrix products, arithmetic and copies ran while one was open for 11% -> 5% of each run, Pallas kernels for 0% -> 0%
where the time goes in v1:
time: 148 us; the launch traced here: 147 us
  blocking collectives  49.9 us (34%)
  waiting for transfers between devices  49.3 us (33%)
  starting transfers between devices  24.7 us (17%)
  other arithmetic  6.81 us (5%)
  matrix products  5.44 us (4%)
  Pallas kernels  5.32 us (4%)
  local copies, waits for them, and re-layouts  4.35 us (3%)
    all_to_all x2, blocking collectives, exchange(): return lax.all_to_all(pieces, axes, split_axis=0, concat_axis=0, tiled=True)  49.9 us
    all_to_all x2, waiting for transfers between devices, exchange(): return lax.all_to_all(pieces, axes, split_axis=0, concat_axis=0, tiled=True)  27.8 us
    ppermute x6, waiting for transfers between devices, partner(): return lax.ppermute(array, axis, [(0, 1), (1, 0)])  21.5 us
    all_to_all x2, starting transfers between devices, exchange(): return lax.all_to_all(pieces, axes, split_axis=0, concat_axis=0, tiled=True)  16.8 us
    ppermute x6, starting transfers between devices, partner(): return lax.ppermute(array, axis, [(0, 1), (1, 0)])  7.94 us
    pallas_call x1, Pallas kernels, project(): pl.pallas_call(project_kernel, out_shape=jax.ShapeDtypeStruct((images, 2...  5.32 us
    dot_general x5, matrix products, dot(): lax.dot_general(a, b, (((a.ndim - 1,), (0,)), ((), ())), preferred_elemen...  5.17 us
  transfers between devices with their start and end apart: 8, of which 5 were waited for; matrix products, arithmetic and copies ran while one was open for 5% of the time, Pallas kernels for 0%

profile of v1, /device:TPU:8, one launch (start us, length us, event | category | flops | bytes accessed | tf_op | source)
XLA Modules:
  0.0 146.8 jit_solution(18046837586964828992)
XLA Ops:
  0.0 1.0 convert_reduce_fusion.1
  1.0 1.0 fusion.31
  2.0 0.9 fusion.33
  2.9 3.1 %collective-permute-start = (bf16[4,6144]{1,0:T(4,128)(2,1)S(1)}, bf16[4,6144]{1,0:T(4,128)(2,1)S(1)}, u32[]{:S(2)}, u32[]{:S(2)}) collective-permute-start(bf16[4,6144]{1,0:T(4,128)(2,1)S(1)} %fusion.33), channel_id=1, source_target_pairs={{0,2},{2,0},{1,3},{3,1},{4,6},{6,4},{5,7},{7,5},{8,10},{10,8},{9,1... | collective-permute-start | bytes 147464 | tf_op jit(solution)/shard_map/ppermute | solution.py:27
  6.0 2.6 %collective-permute-done = bf16[4,6144]{1,0:T(4,128)(2,1)S(1)} collective-permute-done((bf16[4,6144]{1,0:T(4,128)(2,1)S(1)}, bf16[4,6144]{1,0:T(4,128)(2,1)S(1)}, u32[]{:S(2)}, u32[]{:S(2)}) %collective-permute-start) | collective-permute-done | bytes 49184 | tf_op jit(solution)/shard_map/ppermute | solution.py:27
  8.6 0.9 broadcast_select_fusion.2
  9.6 0.1 pad_maximum_fusion.2
  9.6 0.0 copy-start
  9.7 0.0 copy-start.2
  9.7 1.0 broadcast_in_dim.4
  10.7 11.8 %all-to-all-start = ((bf16[32,8,1536]{2,1,0:T(8,128)(2,1)}), bf16[32,8,1536]{2,1,0:T(8,128)(2,1)S(1)}, u32[]{:S(2)}, u32[]{:S(2)}) async-start(bf16[32,8,1536]{2,1,0:T(8,128)(2,1)} %bitcast.2), calls=%async_computation | async-start | bytes 1572864 | tf_op jit(solution)/shard_map/all_to_all | solution.py:31
  22.5 1.6 %collective-permute-start.3 = (bf16[768,768]{1,0:T(8,128)(2,1)S(1)}, bf16[768,768]{1,0:T(8,128)(2,1)}, u32[]{:S(2)}, u32[]{:S(2)}) collective-permute-start(bf16[768,768]{1,0:T(8,128)(2,1)S(1)} %copy-done), channel_id=1, source_target_pairs={{0,128},{128,0},{1,129},{129,1},{2,130},{130,2},{3,131},{131,3},{4... | collective-permute-start | bytes 3538952 | tf_op jit(solution)/shard_map/ppermute | solution.py:27
  24.1 17.7 %all-to-all-done = bf16[32,8,1536]{2,1,0:T(8,128)(2,1)S(1)} async-done(((bf16[32,8,1536]{2,1,0:T(8,128)(2,1)}), bf16[32,8,1536]{2,1,0:T(8,128)(2,1)S(1)}, u32[]{:S(2)}, u32[]{:S(2)}) %all-to-all-start) | async-done | bytes 786464 | tf_op jit(solution)/shard_map/all_to_all | solution.py:31
  42.0 1.6 %collective-permute-start.2 = (bf16[768,384]{1,0:T(8,128)(2,1)S(1)}, bf16[768,384]{1,0:T(8,128)(2,1)S(1)}, u32[]{:S(2)}, u32[]{:S(2)}) collective-permute-start(bf16[768,384]{1,0:T(8,128)(2,1)S(1)} %constant_dynamic-update-slice_fusion.refs_0_), channel_id=1, source_target_pairs={{0,128},{128,0},{1,129},{129,1},{2,130},{130,2},{3,131},{131,3},{4... | collective-permute-start | bytes 1769480 | tf_op jit(solution)/shard_map/ppermute | solution.py:27
  43.6 17.7 %collective-permute-done.2.refs_1_ = bf16[768,384]{1,0:T(8,128)(2,1)S(1)} collective-permute-done((bf16[768,384]{1,0:T(8,128)(2,1)S(1)}, bf16[768,384]{1,0:T(8,128)(2,1)S(1)}, u32[]{:S(2)}, u32[]{:S(2)}) %collective-permute-start.2) | collective-permute-done | bytes 589856 | tf_op jit(solution)/shard_map/ppermute | solution.py:27
  61.3 5.3 %project.1 = bf16[4,128,1152]{2,1,0:T(8,128)(2,1)} custom-call(bf16[4,64,1536]{2,1,0:T(8,128)(2,1)S(1)} %bitcast.23, bf16[4,64,1536]{2,1,0:T(8,128)(2,1)S(1)} %collective-permute-done.1.theirs, bf16[768,384]{1,0:T(8,128)(2,1)S(1)} %constant_dynamic-update-slice_fusion.refs_0_, bf16[768,384]{1,0:T(8,128)(2,1)S(1)} %collective-permute-done.2.refs_1_, ...), custom_call_target="tpu_custom_call" | custom-call | flops 1811939328 | bytes 7340032 | tf_op jit(solution)/shard_map/project/pallas_call | solution.py:77
  66.6 0.0 copy-start.5
  66.6 4.9 %all-to-all-start.1 = ((bf16[4,128,1152]{2,1,0:T(8,128)(2,1)}), bf16[4,128,1152]{2,1,0:T(8,128)(2,1)S(1)}, u32[]{:S(2)}, u32[]{:S(2)}) async-start(bf16[4,128,1152]{2,1,0:T(8,128)(2,1)} %project.1), calls=%async_computation.1 | async-start | bytes 2359296 | tf_op jit(solution)/shard_map/all_to_all | solution.py:31
  71.6 1.3 constant_dynamic-update-slice_fusion.3
  72.9 1.6 %collective-permute-start.4 = (bf16[896,768]{1,0:T(8,128)(2,1)S(1)}, bf16[896,768]{1,0:T(8,128)(2,1)}, u32[]{:S(2)}, u32[]{:S(2)}) collective-permute-start(bf16[896,768]{1,0:T(8,128)(2,1)S(1)} %constant_dynamic-update-slice_fusion.3), channel_id=1, source_target_pairs={{0,128},{128,0},{1,129},{129,1},{2,130},{130,2},{3,131},{131,3},{4... | collective-permute-start | bytes 4128776 | tf_op jit(solution)/shard_map/ppermute | solution.py:27
  75.1 0.0 copy-start.6
  75.2 10.0 %all-to-all-done.1 = bf16[4,128,1152]{2,1,0:T(8,128)(2,1)S(1)} async-done(((bf16[4,128,1152]{2,1,0:T(8,128)(2,1)}), bf16[4,128,1152]{2,1,0:T(8,128)(2,1)S(1)}, u32[]{:S(2)}, u32[]{:S(2)}) %all-to-all-start.1) | async-done | bytes 1179680 | tf_op jit(solution)/shard_map/all_to_all | solution.py:31
  85.2 0.2 convert_reduce_fusion
  85.4 0.1 convert_reduce_fusion.3
  85.5 0.2 fusion.42
  85.7 0.3 fusion.56
  86.0 0.2 convolution_convert_fusion
  86.3 0.1 copy.16
  86.4 0.9 fusion.21
  87.3 0.1 broadcast_in_dim.5
  87.4 13.9 %all_to_all.20 = bf16[4,128,896]{2,1,0:T(8,128)(2,1)S(1)} all-to-all(bf16[4,128,896]{2,1,0:T(8,128)(2,1)S(1)} %broadcast_in_dim.5), channel_id=1, replica_groups=mesh['xl'=2,'y'=4,'z'=8,'xh'=2,'c'=2] {'y'}, dimensions={0} | all-to-all | bytes 1835008 | tf_op jit(solution)/shard_map/all_to_all | solution.py:31
  101.2 0.6 fusion.9
  101.8 1.3 collective-permute-done.4
  103.1 1.9 %fusion.12 = bf16[4,64,768]{2,1,0:T(8,128)(2,1)S(1)} fusion(bf16[896,768]{1,0:T(8,128)(2,1)} %collective-permute-done.4, bf16[4,128,896]{2,1,0:T(8,128)(2,1)S(1)} %all_to_all.20), kind=kOutput, calls=%fused_computation.12 | convolution fusion | flops 352518144 | bytes 2228224 | tf_op jit(solution)/shard_map/dot_general | solution.py:35
  105.0 0.1 pad_maximum_fusion
  105.1 0.1 collective-permute-start.5
  105.2 0.6 fusion.7
  105.7 1.9 %fusion.3 = f32[4,64,768]{2,1,0:T(8,128)S(1)} fusion(bf16[896,768]{1,0:T(8,128)(2,1)} %collective-permute-done.4, bf16[4,128,896]{2,1,0:T(8,128)(2,1)S(1)} %all_to_all.20), kind=kOutput, calls=%fused_computation.5 | convolution fusion | flops 352321536 | bytes 2621440 | tf_op jit(solution)/shard_map/dot_general | solution.py:35
  107.7 0.2 fusion
  107.8 0.2 reshape.63
  108.0 36.0 %all_to_all.21 = bf16[64,4,1536]{2,1,0:T(4,128)(2,1)S(1)} all-to-all(bf16[64,4,1536]{2,1,0:T(4,128)(2,1)S(1)} %reshape.63), channel_id=1, replica_groups=mesh['xl'=2,'y'=4,'z'=8,'xh'=2,'c'=2] {'y','z','xh'}, dimensions={0} | all-to-all | bytes 1572864 | tf_op jit(solution)/shard_map/all_to_all | solution.py:31
  144.0 1.0 reshape.65
  145.0 0.0 copy-start.1
  145.0 0.5 reduce_sum.89
  145.5 0.4 rev.9
  145.9 0.1 broadcast_select_fusion
  146.0 0.1 reshape.64
  146.1 0.6 fusion.34
  (28 shorter events, 0.4 us)
Async XLA Ops:
  2.9 5.7 %collective-permute-start = (bf16[4,6144]{1,0:T(4,128)(2,1)S(1)}, bf16[4,6144]{1,0:T(4,128)(2,1)S(1)}, u32[]{:S(2)}, u32[]{:S(2)}) collective-permute-start(bf16[4,6144]{1,0:T(4,128)(2,1)S(1)} %fusion.33), channel_id=1, source_target_pairs={{0,2},{2,0},{1,3},{3,1},{4,6},{6,4},{5,7},{7,5},{8,10},{10,8},{9,1... | collective-permute-start | bytes 147464 | tf_op jit(solution)/shard_map/ppermute | solution.py:27
  9.6 12.9 %copy-start = (bf16[768,768]{1,0:T(8,128)(2,1)S(1)}, bf16[768,768]{1,0:T(8,128)(2,1)}, u32[]{:S(2)}) copy-start(bf16[768,768]{1,0:T(8,128)(2,1)} %refs_2_.1) | copy-start | bytes 3538948
  9.7 14.5 %copy-start.2 = (bf16[768,128]{1,0:T(8,128)(2,1)S(1)}, bf16[768,128]{1,0:T(8,128)(2,1)}, u32[]{:S(2)}) copy-start(bf16[768,128]{1,0:T(8,128)(2,1)} %param.12) | copy-start | bytes 589828
  9.7 32.2 %copy-start.3 = (bf16[768,128]{1,0:T(8,128)(2,1)S(1)}, bf16[768,128]{1,0:T(8,128)(2,1)}, u32[]{:S(2)}) copy-start(bf16[768,128]{1,0:T(8,128)(2,1)} %param.13) | copy-start | bytes 589828
  10.7 31.3 %copy-start.4 = (bf16[768,128]{1,0:T(8,128)(2,1)S(1)}, bf16[768,128]{1,0:T(8,128)(2,1)}, u32[]{:S(2)}) copy-start(bf16[768,128]{1,0:T(8,128)(2,1)} %param.14) | copy-start | bytes 589828
  10.7 31.2 %all-to-all-start = ((bf16[32,8,1536]{2,1,0:T(8,128)(2,1)}), bf16[32,8,1536]{2,1,0:T(8,128)(2,1)S(1)}, u32[]{:S(2)}, u32[]{:S(2)}) async-start(bf16[32,8,1536]{2,1,0:T(8,128)(2,1)} %bitcast.2), calls=%async_computation | async-start | bytes 1572864 | tf_op jit(solution)/shard_map/all_to_all | solution.py:31
  22.5 38.7 %collective-permute-start.3 = (bf16[768,768]{1,0:T(8,128)(2,1)S(1)}, bf16[768,768]{1,0:T(8,128)(2,1)}, u32[]{:S(2)}, u32[]{:S(2)}) collective-permute-start(bf16[768,768]{1,0:T(8,128)(2,1)S(1)} %copy-done), channel_id=1, source_target_pairs={{0,128},{128,0},{1,129},{129,1},{2,130},{130,2},{3,131},{131,3},{4... | collective-permute-start | bytes 3538952 | tf_op jit(solution)/shard_map/ppermute | solution.py:27
  41.9 19.4 %collective-permute-start.1 = (bf16[4,64,1536]{2,1,0:T(8,128)(2,1)S(1)}, bf16[4,64,1536]{2,1,0:T(8,128)(2,1)S(1)}, u32[]{:S(2)}, u32[]{:S(2)}) collective-permute-start(bf16[4,64,1536]{2,1,0:T(8,128)(2,1)S(1)} %bitcast.22), channel_id=1, source_target_pairs={{0,1},{1,0},{2,3},{3,2},{4,5},{5,4},{6,7},{7,6},{8,9},{9,8},{10,11... | collective-permute-start | bytes 2359304 | tf_op jit(solution)/shard_map/ppermute | solution.py:27
  42.0 19.2 %collective-permute-start.2 = (bf16[768,384]{1,0:T(8,128)(2,1)S(1)}, bf16[768,384]{1,0:T(8,128)(2,1)S(1)}, u32[]{:S(2)}, u32[]{:S(2)}) collective-permute-start(bf16[768,384]{1,0:T(8,128)(2,1)S(1)} %constant_dynamic-update-slice_fusion.refs_0_), channel_id=1, source_target_pairs={{0,128},{128,0},{1,129},{129,1},{2,130},{130,2},{3,131},{131,3},{4... | collective-permute-start | bytes 1769480 | tf_op jit(solution)/shard_map/ppermute | solution.py:27
  66.6 5.0 %copy-start.5 = (bf16[128,768]{1,0:T(8,128)(2,1)S(1)}, bf16[128,768]{1,0:T(8,128)(2,1)}, u32[]{:S(2)}) copy-start(bf16[128,768]{1,0:T(8,128)(2,1)} %param.17) | copy-start | bytes 589828
  66.6 18.6 %all-to-all-start.1 = ((bf16[4,128,1152]{2,1,0:T(8,128)(2,1)}), bf16[4,128,1152]{2,1,0:T(8,128)(2,1)S(1)}, u32[]{:S(2)}, u32[]{:S(2)}) async-start(bf16[4,128,1152]{2,1,0:T(8,128)(2,1)} %project.1), calls=%async_computation.1 | async-start | bytes 2359296 | tf_op jit(solution)/shard_map/all_to_all | solution.py:31
  72.9 30.2 %collective-permute-start.4 = (bf16[896,768]{1,0:T(8,128)(2,1)S(1)}, bf16[896,768]{1,0:T(8,128)(2,1)}, u32[]{:S(2)}, u32[]{:S(2)}) collective-permute-start(bf16[896,768]{1,0:T(8,128)(2,1)S(1)} %constant_dynamic-update-slice_fusion.3), channel_id=1, source_target_pairs={{0,128},{128,0},{1,129},{129,1},{2,130},{130,2},{3,131},{131,3},{4... | collective-permute-start | bytes 4128776 | tf_op jit(solution)/shard_map/ppermute | solution.py:27
  75.1 11.2 %copy-start.6 = (f32[768]{0:T(1024)S(1)}, f32[768]{0:T(1024)}, u32[]{:S(2)}) copy-start(f32[768]{0:T(1024)} %param.16) | copy-start | bytes 9220
  105.1 2.6 %collective-permute-start.5 = (bf16[4,64,1536]{2,1,0:T(8,128)(2,1)S(1)}, bf16[4,64,1536]{2,1,0:T(8,128)(2,1)S(1)}, u32[]{:S(2)}, u32[]{:S(2)}) collective-permute-start(bf16[4,64,1536]{2,1,0:T(8,128)(2,1)S(1)} %pad_maximum_fusion), channel_id=1, source_target_pairs={{0,1},{1,0},{2,3},{3,2},{4,5},{5,4},{6,7},{7,6},{8,9},{9,8},{10,11... | collective-permute-start | bytes 2359304 | tf_op jit(solution)/shard_map/ppermute | solution.py:27
  145.0 1.1 copy-start.1

commit v2 on v0

v2 whole, which is shorter than its diff:
```python
import functools
import math

import jax
import jax.numpy as jnp
from jax import lax
from jax.experimental import pallas as pl
from jax.experimental.pallas import tpu as pltpu
from jax.sharding import Mesh
from jax.sharding import PartitionSpec as P


HEAD = 128
DP = ("xl", "y")
MP = ("z", "xh", "c")
ALL = DP + MP
BF = jnp.bfloat16
F32 = jnp.float32
ANY = pl.BlockSpec(memory_space=pl.ANY)
VMEM = pl.BlockSpec(memory_space=pltpu.VMEM)


def normalize(values):
    center = values - jnp.mean(values, axis=-1, keepdims=True)
    spread = jnp.mean(center * center, axis=-1, keepdims=True)
    return center * lax.rsqrt(spread + 1e-06)


def partner(array, axis):
    return lax.ppermute(array, axis, [(0, 1), (1, 0)])


def exchange(pieces, axes):
    return lax.all_to_all(pieces, axes, split_axis=0, concat_axis=0, tiled=True)


def dot(a, b):
    return lax.dot_general(a, b, (((a.ndim - 1,), (0,)), ((), ())), preferred_element_type=F32)


def params(mib):
    return pltpu.CompilerParams(vmem_limit_bytes=mib * 1024 * 1024)


def cost(flops, moved):
    return pl.CostEstimate(flops=flops, bytes_accessed=moved, transcendentals=0)


def spread_kernel(n_y, n_z, own, beside, gain, out):
    _, width = own.shape
    cols = width // (2 * n_y)
    mine, theirs = own[...].astype(F32), beside[...].astype(F32)
    first = lax.axis_index("xh") == 0
    rows = jnp.concatenate(
        (jnp.where(first, mine, theirs), jnp.where(first, theirs, mine)), axis=0
    )
    normed = normalize(rows) * gain[...]
    lower = lax.axis_index("xl") == 0
    for y in range(n_y):
        a = normed[:, y * cols : (y + 1) * cols]
        b = normed[:, (n_y + y) * cols : (n_y + y + 1) * cols]
        left = jnp.where(lower, a, b).astype(BF)
        right = jnp.where(lower, b, a).astype(BF)
        for z in range(n_z):
            out[y * n_z + z, :, :cols] = left
            out[y * n_z + z, :, cols:] = right


def spread(tokens, beside, gain, n_y, n_z):
    count, width = tokens.shape
    return pl.pallas_call(
        functools.partial(spread_kernel, n_y, n_z),
        out_shape=jax.ShapeDtypeStruct((n_y * n_z, 2 * count, width // n_y), BF),
        in_specs=[VMEM] * 3,
        out_specs=VMEM,
        compiler_params=params(8),
        cost_estimate=cost(20 * count * width, 2 * 1024 * 1024),
        name="normed_pieces",
    )(tokens, beside, gain.reshape(1, width))


def project_kernel(before, chunk, *refs):
    count = 4 + before
    sources, out = refs[:count], refs[count]
    kept, sems = refs[count + 1 : count + 5], refs[count + 5]
    done = []
    if before:
        width = sources[4].shape[-1]
        done = [
            pltpu.make_async_copy(
                sources[4], out.at[:, :, out.shape[-1] - width :], sems.at[4]
            )
        ]
    copies = [pltpu.make_async_copy(sources[n], kept[n], sems.at[n]) for n in range(4)]
    for n in (0, 2, 3, 1):
        copies[n].start()
    for copy in done:
        copy.start()
    images, half, width = kept[0].shape
    cols = width // 2
    for n in (0, 2, 3):
        copies[n].wait()
    w, w_p = kept[2], kept[3]
    for part in range(2):
        if part:
            copies[1].wait()
        rows = kept[part][...].reshape(images * half, width)
        for n in range(w.shape[1] // chunk):
            at = slice(n * chunk, (n + 1) * chunk)
            value = dot(rows[:, :cols], w[:, at]) + dot(rows[:, cols:], w_p[:, at])
            out[:, part * half : (part + 1) * half, at] = value.astype(BF).reshape(
                images, half, chunk
            )
    for copy in done:
        copy.wait()


def project(mine, theirs, weights, weights_p, before=None):
    images, half, width = mine.shape
    columns = weights.shape[1] + (0 if before is None else before.shape[-1])
    arrays = (mine, theirs, weights, weights_p) + (() if before is None else (before,))
    return pl.pallas_call(
        functools.partial(project_kernel, int(before is not None), 384),
        out_shape=jax.ShapeDtypeStruct((images, 2 * half, columns), BF),
        in_specs=[ANY] * len(arrays),
        out_specs=VMEM,
        scratch_shapes=[pltpu.VMEM(a.shape, BF) for a in arrays[:4]]
        + [pltpu.SemaphoreType.DMA((5,))],
        compiler_params=params(16),
        cost_estimate=cost(4 * images * half * width * weights.shape[1], 5 * 1024 * 1024),
        name="project" if before is None else "project_more",
    )(*arrays)


def output_kernel(part, features, w_own, w_other, out, rows, kept_own, kept_other, sems):
    images, half, width = rows.shape
    cols = kept_own.shape[1]
    copies = [
        pltpu.make_async_copy(
            features.at[:, part * half : (part + 1) * half], rows, sems.at[0]
        ),
        pltpu.make_async_copy(w_own, kept_own, sems.at[1]),
        pltpu.make_async_copy(w_other, kept_other, sems.at[2]),
    ]
    for copy in copies:
        copy.start()
    copies[0].wait()
    left = rows[...].reshape(images * half, width)
    for n, kept in enumerate((kept_own, kept_other)):
        copies[n + 1].wait()
        for m in range(2):
            at = slice(m * cols // 2, (m + 1) * cols // 2)
            value = dot(left, kept[:, at]).astype(out.dtype).reshape(images, half, cols // 2)
            out[:, :, n * cols + m * cols // 2 : n * cols + (m + 1) * cols // 2] = value


def output(features, w_own, w_other, part, kind):
    images, patches, width = features.shape
    half, cols = patches // 2, w_own.shape[1]
    return pl.pallas_call(
        functools.partial(output_kernel, part),
        out_shape=jax.ShapeDtypeStruct((images, half, 2 * cols), kind),
        in_specs=[ANY] * 3,
        out_specs=VMEM,
        scratch_shapes=[
            pltpu.VMEM((images, half, width), BF),
            pltpu.VMEM(w_own.shape, BF),
            pltpu.VMEM(w_other.shape, BF),
            pltpu.SemaphoreType.DMA((3,)),
        ],
        compiler_params=params(16),
        cost_estimate=cost(4 * images * half * width * cols, 4 * 1024 * 1024),
        name="output_sent" if part else "output_kept",
    )(features, w_own, w_other)


def finish_kernel(n_y, arrived, tokens, out):
    pieces, _, width = arrived.shape
    cols = width // 2
    lower = lax.axis_index("xl") == 0
    for y in range(n_y):
        at = slice(y * pieces // n_y, (y + 1) * pieces // n_y)
        total = arrived[at].astype(F32).sum(axis=0)
        left, right = total[:, :cols], total[:, cols:]
        for n, value in enumerate(
            (jnp.where(lower, left, right), jnp.where(lower, right, left))
        ):
            to = slice((n * n_y + y) * cols, (n * n_y + y + 1) * cols)
            out[:, to] = (tokens[:, to].astype(F32) + value).astype(BF)


def finish(arrived, tokens, n_y):
    return pl.pallas_call(
        functools.partial(finish_kernel, n_y),
        out_shape=jax.ShapeDtypeStruct(tokens.shape, BF),
        in_specs=[VMEM] * 2,
        out_specs=VMEM,
        compiler_params=params(8),
        cost_estimate=cost(arrived.size, 2 * 1024 * 1024),
        name="finish",
    )(arrived, tokens)


def block(
    tokens, norm_gain, w_query, w_key, w_value, w_inner, bias_inner, w_attn_out, w_outer, temper
):
    count = tokens.shape[0]
    n_y, n_z, n_xh = (lax.axis_size(a) for a in ("y", "z", "xh"))
    beside = partner(tokens, "xh")
    w_qkv = jnp.concatenate((w_query, w_key, w_value), axis=1)
    w_out = jnp.concatenate((w_attn_out, w_outer), axis=0)
    w_inner_p = partner(w_inner, "xl")
    w_qkv_p = partner(w_qkv, "xl")
    w_out_p = partner(w_out, "xl")
    pieces = spread(tokens, beside, norm_gain, n_y, n_z)
    mine = exchange(pieces, ("y", "z"))
    mine = mine.reshape(n_y, -1, mine.shape[-1])
    theirs = partner(mine, "c")
    partial = project(mine, theirs, w_inner, w_inner_p)
    partial = project(mine, theirs, w_qkv, w_qkv_p, partial)
    sums = exchange(partial, "y").astype(F32).sum(axis=0)
    scale = temper / math.sqrt(HEAD)
    query_norm = normalize(sums[:, :HEAD].astype(BF).astype(F32)).astype(BF)
    key_norm = normalize(sums[:, HEAD : 2 * HEAD].astype(BF).astype(F32)).astype(BF)
    value = sums[:, 2 * HEAD : 3 * HEAD].astype(BF)
    scores = jnp.einsum("qc,kc->qk", query_norm, key_norm, preferred_element_type=F32)
    scores = scores * scale
    probs = jax.nn.softmax(scores, axis=-1).astype(BF)
    mixed = dot(probs, value).astype(BF)
    inner = sums[:, 3 * HEAD :] + bias_inner
    activ = jax.nn.gelu(inner, approximate=False).astype(BF)
    features = jnp.concatenate((mixed, activ), axis=1)
    features = exchange(jnp.broadcast_to(features, (n_y, *features.shape)), "y")
    sent = partner(output(features, w_out, w_out_p, 1, BF), "c")
    kept = output(features, w_out, w_out_p, 0, F32)
    summed = (kept + sent.astype(F32)).astype(BF)
    pieces = summed.reshape(n_y * n_z * n_xh, count, summed.shape[-1])
    arrived = exchange(pieces, ("y", "z", "xh"))
    return finish(arrived, tokens, n_y)


def solution(mesh):
    finer = Mesh(mesh.devices.reshape(2, 4, 8, 2, 2), ALL)
    return jax.shard_map(
        block,
        mesh=finer,
        in_specs=(
            P(ALL, None),
            P(),
            P(DP, MP),
            P(DP, MP),
            P(DP, MP),
            P(DP, MP),
            P(MP),
            P(MP, DP),
            P(MP, DP),
            P(MP),
        ),
        out_specs=P(ALL, None),
        check_vma=False,
    )
```

time: 151 us -> 141 us (0.934)
  blocking collectives: 49.8 us -> 34.1 us
  matrix products: 13.4 us -> 0.48 us
  waiting for transfers between devices: 43.7 us -> 56.4 us
  Pallas kernels: 0 us -> 12 us
  other arithmetic: 6.79 us -> 1.61 us
    all_to_all x2 -> x1, blocking collectives: 49.8 us -> 34.1 us  [exchange(): return lax.all_to_all(pieces, axes, split_axis=0, concat_axis=0, tiled=True)]
    dot_general x9 -> x1, matrix products: 13.2 us -> 0.21 us  [dot(): lax.dot_general(a, b, (((a.ndim - 1,), (0,)), ((), ())), preferred_elemen...]
    pallas_call x0 -> x6, Pallas kernels: none -> 12 us  [the longest x2 5.23 us: project(): pl.pallas_call(functools.partial(project_kernel, int(before is not None),...]
    ppermute x6, waiting for transfers between devices: 18.8 us -> 26.7 us  [partner(): return lax.ppermute(array, axis, [(0, 1), (1, 0)])]
    all_to_all x3, waiting for transfers between devices: 24.9 us -> 29.7 us  [exchange(): return lax.all_to_all(pieces, axes, split_axis=0, concat_axis=0, tiled=True)]
    convert_element_type x3 -> x1, other arithmetic: 1.71 us -> 0.19 us  [block(): summed = (kept + sent.astype(F32)).astype(BF)]
  transfers between devices with their start and end apart: 9 -> 9, of which waited for: 5 -> 7; matrix products, arithmetic and copies ran while one was open for 11% -> 4% of each run, Pallas kernels for 0% -> 3%
where the time goes in v2:
time: 141 us; the launch traced here: 140 us
  waiting for transfers between devices  56.4 us (40%)
  blocking collectives  34.1 us (24%)
  starting transfers between devices  29.6 us (21%)
  Pallas kernels  12 us (9%)
  local copies, waits for them, and re-layouts  5.29 us (4%)
  other arithmetic  1.61 us (1%)
    all_to_all x1, blocking collectives, exchange(): return lax.all_to_all(pieces, axes, split_axis=0, concat_axis=0, tiled=True)  34.1 us
    all_to_all x3, waiting for transfers between devices, exchange(): return lax.all_to_all(pieces, axes, split_axis=0, concat_axis=0, tiled=True)  29.7 us
    ppermute x6, waiting for transfers between devices, partner(): return lax.ppermute(array, axis, [(0, 1), (1, 0)])  26.7 us
    all_to_all x3, starting transfers between devices, exchange(): return lax.all_to_all(pieces, axes, split_axis=0, concat_axis=0, tiled=True)  21.6 us
    ppermute x6, starting transfers between devices, partner(): return lax.ppermute(array, axis, [(0, 1), (1, 0)])  8.04 us
    pallas_call x2, Pallas kernels, project(): pl.pallas_call(functools.partial(project_kernel, int(before is not None),...  5.23 us
    pallas_call x2, Pallas kernels, output(): pl.pallas_call(functools.partial(output_kernel, part), out_shape=jax.Shap...  4.58 us
  transfers between devices with their start and end apart: 9, of which 7 were waited for; matrix products, arithmetic and copies ran while one was open for 4% of the time, Pallas kernels for 3%

profile of v2, /device:TPU:8, one launch (start us, length us, event | category | flops | bytes accessed | tf_op | source)
XLA Modules:
  0.0 140.4 jit_solution(2724885288907837882)
XLA Ops:
  0.0 3.0 %collective-permute-start = (bf16[4,6144]{1,0:T(4,128)(2,1)}, bf16[4,6144]{1,0:T(4,128)(2,1)S(1)}, u32[]{:S(2)}, u32[]{:S(2)}) collective-permute-start(bf16[4,6144]{1,0:T(4,128)(2,1)} %tokens.1), channel_id=1, source_target_pairs={{0,2},{2,0},{1,3},{3,1},{4,6},{6,4},{5,7},{7,5},{8,10},{10,8},{9,1... | collective-permute-start | bytes 147464 | tf_op jit(solution)/shard_map/ppermute | solution.py:30
  3.0 2.8 %collective-permute-done.beside = bf16[4,6144]{1,0:T(4,128)(2,1)S(1)} collective-permute-done((bf16[4,6144]{1,0:T(4,128)(2,1)}, bf16[4,6144]{1,0:T(4,128)(2,1)S(1)}, u32[]{:S(2)}, u32[]{:S(2)}) %collective-permute-start) | collective-permute-done | bytes 49184 | tf_op jit(solution)/shard_map/ppermute | solution.py:30
  5.8 0.8 copy-done.1
  6.6 0.7 copy-done.3
  7.3 1.2 normed_pieces.1
  8.6 11.7 %all-to-all-start = ((bf16[32,8,1536]{2,1,0:T(8,128)(2,1)}), bf16[32,8,1536]{2,1,0:T(8,128)(2,1)S(1)}, u32[]{:S(2)}, u32[]{:S(2)}) async-start(bf16[32,8,1536]{2,1,0:T(8,128)(2,1)} %normed_pieces.1), calls=%async_computation | async-start | bytes 1572864 | tf_op jit(solution)/shard_map/all_to_all | solution.py:34
  20.3 0.0 copy-done
  20.3 1.6 %collective-permute-start.3 = (bf16[768,768]{1,0:T(8,128)(2,1)S(1)}, bf16[768,768]{1,0:T(8,128)(2,1)S(1)}, u32[]{:S(2)}, u32[]{:S(2)}) collective-permute-start(bf16[768,768]{1,0:T(8,128)(2,1)S(1)} %copy-done), channel_id=1, source_target_pairs={{0,128},{128,0},{1,129},{129,1},{2,130},{130,2},{3,131},{131,3},{4... | collective-permute-start | bytes 3538952 | tf_op jit(solution)/shard_map/ppermute | solution.py:30
  21.9 17.8 %all-to-all-done = bf16[32,8,1536]{2,1,0:T(8,128)(2,1)S(1)} async-done(((bf16[32,8,1536]{2,1,0:T(8,128)(2,1)}), bf16[32,8,1536]{2,1,0:T(8,128)(2,1)S(1)}, u32[]{:S(2)}, u32[]{:S(2)}) %all-to-all-start) | async-done | bytes 786464 | tf_op jit(solution)/shard_map/all_to_all | solution.py:34
  39.7 0.0 collective-permute-start.1
  39.7 0.0 copy-done.4
  39.7 0.0 copy-done.5
  39.8 1.0 constant_dynamic-update-slice_fusion.refs_2_
  40.8 1.6 %collective-permute-start.2 = (bf16[768,384]{1,0:T(8,128)(2,1)S(1)}, bf16[768,384]{1,0:T(8,128)(2,1)S(1)}, u32[]{:S(2)}, u32[]{:S(2)}) collective-permute-start(bf16[768,384]{1,0:T(8,128)(2,1)S(1)} %constant_dynamic-update-slice_fusion.refs_2_), channel_id=1, source_target_pairs={{0,128},{128,0},{1,129},{129,1},{2,130},{130,2},{3,131},{131,3},{4... | collective-permute-start | bytes 1769480 | tf_op jit(solution)/shard_map/ppermute | solution.py:30
  42.3 6.5 %collective-permute-done.3.refs_3_ = bf16[768,768]{1,0:T(8,128)(2,1)S(1)} collective-permute-done((bf16[768,768]{1,0:T(8,128)(2,1)S(1)}, bf16[768,768]{1,0:T(8,128)(2,1)S(1)}, u32[]{:S(2)}, u32[]{:S(2)}) %collective-permute-start.3) | collective-permute-done | bytes 1179680 | tf_op jit(solution)/shard_map/ppermute | solution.py:30
  48.8 0.0 collective-permute-done.1.refs_1_
  48.8 2.6 %project.1.refs_4_ = bf16[4,128,768]{2,1,0:T(8,128)(2,1)S(1)} custom-call(bf16[4,64,1536]{2,1,0:T(8,128)(2,1)S(1)} %bitcast.4, bf16[4,64,1536]{2,1,0:T(8,128)(2,1)S(1)} %collective-permute-done.1.refs_1_, bf16[768,768]{1,0:T(8,128)(2,1)S(1)} %copy-done, bf16[768,768]{1,0:T(8,128)(2,1)S(1)} %collective-permute-done.3.refs_3_), custom_call_target="tpu_custom_call" | custom-call | flops 1207959552 | bytes 5242880 | tf_op jit(solution)/shard_map/project/pallas_call | solution.py:122
  51.4 7.6 %collective-permute-done.2.refs_3_ = bf16[768,384]{1,0:T(8,128)(2,1)S(1)} collective-permute-done((bf16[768,384]{1,0:T(8,128)(2,1)S(1)}, bf16[768,384]{1,0:T(8,128)(2,1)S(1)}, u32[]{:S(2)}, u32[]{:S(2)}) %collective-permute-start.2) | collective-permute-done | bytes 589856 | tf_op jit(solution)/shard_map/ppermute | solution.py:30
  59.0 2.6 %project_more.1 = bf16[4,128,1152]{2,1,0:T(8,128)(2,1)} custom-call(bf16[4,64,1536]{2,1,0:T(8,128)(2,1)S(1)} %bitcast.5, bf16[4,64,1536]{2,1,0:T(8,128)(2,1)S(1)} %collective-permute-done.1.refs_1_, bf16[768,384]{1,0:T(8,128)(2,1)S(1)} %constant_dynamic-update-slice_fusion.refs_2_, bf16[768,384]{1,0:T(8,128)(2,1)S(1)} %collective-permute-done.2.refs_3_, ...), custom_call_target="tpu_custom_call" | custom-call | flops 603979776 | bytes 5242880 | tf_op jit(solution)/shard_map/project_more/pallas_call | solution.py:122
  61.7 0.0 copy-start.6
  61.7 4.9 %all-to-all-start.1 = ((bf16[4,128,1152]{2,1,0:T(8,128)(2,1)}), bf16[4,128,1152]{2,1,0:T(8,128)(2,1)S(1)}, u32[]{:S(2)}, u32[]{:S(2)}) async-start(bf16[4,128,1152]{2,1,0:T(8,128)(2,1)} %project_more.1), calls=%async_computation.1 | async-start | bytes 2359296 | tf_op jit(solution)/shard_map/all_to_all | solution.py:34
  66.6 0.0 copy-done.6
  66.6 1.3 constant_dynamic-update-slice_fusion.3.w_own
  68.0 1.6 %collective-permute-start.4 = (bf16[896,768]{1,0:T(8,128)(2,1)S(1)}, bf16[896,768]{1,0:T(8,128)(2,1)}, u32[]{:S(2)}, u32[]{:S(2)}) collective-permute-start(bf16[896,768]{1,0:T(8,128)(2,1)S(1)} %constant_dynamic-update-slice_fusion.3.w_own), channel_id=1, source_target_pairs={{0,128},{128,0},{1,129},{129,1},{2,130},{130,2},{3,131},{131,3},{4... | collective-permute-start | bytes 4128776 | tf_op jit(solution)/shard_map/ppermute | solution.py:30
  70.2 0.0 copy-start.7
  70.2 10.9 %all-to-all-done.1 = bf16[4,128,1152]{2,1,0:T(8,128)(2,1)S(1)} async-done(((bf16[4,128,1152]{2,1,0:T(8,128)(2,1)}), bf16[4,128,1152]{2,1,0:T(8,128)(2,1)S(1)}, u32[]{:S(2)}, u32[]{:S(2)}) %all-to-all-start.1) | async-done | bytes 1179680 | tf_op jit(solution)/shard_map/all_to_all | solution.py:34
  81.1 0.2 convert_reduce_fusion
  81.3 0.1 convert_reduce_fusion.2
  81.5 0.2 fusion.16
  81.7 0.3 fusion.30
  82.0 0.2 convolution_convert_fusion
  82.2 0.1 copy.11
  82.3 0.0 copy-done.7
  82.3 0.9 fusion.2
  83.2 1.0 broadcast_in_dim.2
  84.2 4.9 %all-to-all-start.2 = ((bf16[4,128,896]{2,1,0:T(8,128)(2,1)}), bf16[4,128,896]{2,1,0:T(8,128)(2,1)S(1)}, u32[]{:S(2)}, u32[]{:S(2)}) async-start(bf16[4,128,896]{2,1,0:T(8,128)(2,1)} %broadcast_in_dim.2), calls=%async_computation.2 | async-start | bytes 1835008 | tf_op jit(solution)/shard_map/all_to_all | solution.py:34
  89.2 9.9 %collective-permute-done.4.w_other = bf16[896,768]{1,0:T(8,128)(2,1)} collective-permute-done((bf16[896,768]{1,0:T(8,128)(2,1)S(1)}, bf16[896,768]{1,0:T(8,128)(2,1)}, u32[]{:S(2)}, u32[]{:S(2)}) %collective-permute-start.4) | collective-permute-done | bytes 1376288 | tf_op jit(solution)/shard_map/ppermute | solution.py:30
  99.0 1.0 all-to-all-done.2.features
  100.0 2.3 %output_sent.1 = bf16[4,64,1536]{2,1,0:T(8,128)(2,1)S(1)} custom-call(bf16[4,128,896]{2,1,0:T(8,128)(2,1)S(1)} %all-to-all-done.2.features, bf16[896,768]{1,0:T(8,128)(2,1)S(1)} %constant_dynamic-update-slice_fusion.3.w_own, bf16[896,768]{1,0:T(8,128)(2,1)} %collective-permute-done.4.w_other), custom_call_target="tpu_custom_call" | custom-call | flops 704643072 | bytes 4194304 | tf_op jit(solution)/shard_map/output_sent/pallas_call | solution.py:160
  102.3 0.3 collective-permute-start.5
  102.6 2.3 %output_kept.1 = f32[4,64,1536]{2,1,0:T(8,128)S(1)} custom-call(bf16[4,128,896]{2,1,0:T(8,128)(2,1)S(1)} %all-to-all-done.2.features, bf16[896,768]{1,0:T(8,128)(2,1)S(1)} %constant_dynamic-update-slice_fusion.3.w_own, bf16[896,768]{1,0:T(8,128)(2,1)} %collective-permute-done.4.w_other), custom_call_target="tpu_custom_call" | custom-call | flops 704643072 | bytes 4194304 | tf_op jit(solution)/shard_map/output_kept/pallas_call | solution.py:160
  104.9 0.0 collective-permute-done.5
  104.9 0.2 add_convert_fusion
  105.1 0.0 copy-start.2
  105.1 0.2 reshape.39
  105.3 34.1 %all_to_all.20.arrived = bf16[64,4,1536]{2,1,0:T(4,128)(2,1)S(1)} all-to-all(bf16[64,4,1536]{2,1,0:T(4,128)(2,1)S(1)} %reshape.39), channel_id=1, replica_groups=mesh['xl'=2,'y'=4,'z'=8,'xh'=2,'c'=2] {'y','z','xh'}, dimensions={0} | all-to-all | bytes 1572864 | tf_op jit(solution)/shard_map/all_to_all | solution.py:34
  139.4 0.0 copy-done.2
  139.4 1.0 finish.1
  (14 shorter events, 0.2 us)
Async XLA Ops:
  0.0 20.3 %copy-start = (bf16[768,768]{1,0:T(8,128)(2,1)S(1)}, bf16[768,768]{1,0:T(8,128)(2,1)}, u32[]{:S(2)}) copy-start(bf16[768,768]{1,0:T(8,128)(2,1)} %refs_2_.1) | copy-start | bytes 3538948
  0.0 5.8 %collective-permute-start = (bf16[4,6144]{1,0:T(4,128)(2,1)}, bf16[4,6144]{1,0:T(4,128)(2,1)S(1)}, u32[]{:S(2)}, u32[]{:S(2)}) collective-permute-start(bf16[4,6144]{1,0:T(4,128)(2,1)} %tokens.1), channel_id=1, source_target_pairs={{0,2},{2,0},{1,3},{3,1},{4,6},{6,4},{5,7},{7,5},{8,10},{10,8},{9,1... | collective-permute-start | bytes 147464 | tf_op jit(solution)/shard_map/ppermute | solution.py:30
  5.8 0.8 copy-start.1
  6.6 0.7 copy-start.3
  7.3 32.3 %copy-start.4 = (bf16[768,128]{1,0:T(8,128)(2,1)S(1)}, bf16[768,128]{1,0:T(8,128)(2,1)}, u32[]{:S(2)}) copy-start(bf16[768,128]{1,0:T(8,128)(2,1)} %param.12) | copy-start | bytes 589828
  7.3 32.4 %copy-start.5 = (bf16[768,128]{1,0:T(8,128)(2,1)S(1)}, bf16[768,128]{1,0:T(8,128)(2,1)}, u32[]{:S(2)}) copy-start(bf16[768,128]{1,0:T(8,128)(2,1)} %param.13) | copy-start | bytes 589828
  8.6 31.1 %all-to-all-start = ((bf16[32,8,1536]{2,1,0:T(8,128)(2,1)}), bf16[32,8,1536]{2,1,0:T(8,128)(2,1)S(1)}, u32[]{:S(2)}, u32[]{:S(2)}) async-start(bf16[32,8,1536]{2,1,0:T(8,128)(2,1)} %normed_pieces.1), calls=%async_computation | async-start | bytes 1572864 | tf_op jit(solution)/shard_map/all_to_all | solution.py:34
  20.3 28.5 %collective-permute-start.3 = (bf16[768,768]{1,0:T(8,128)(2,1)S(1)}, bf16[768,768]{1,0:T(8,128)(2,1)S(1)}, u32[]{:S(2)}, u32[]{:S(2)}) collective-permute-start(bf16[768,768]{1,0:T(8,128)(2,1)S(1)} %copy-done), channel_id=1, source_target_pairs={{0,128},{128,0},{1,129},{129,1},{2,130},{130,2},{3,131},{131,3},{4... | collective-permute-start | bytes 3538952 | tf_op jit(solution)/shard_map/ppermute | solution.py:30
  39.7 9.2 %collective-permute-start.1 = (bf16[4,64,1536]{2,1,0:T(8,128)(2,1)S(1)}, bf16[4,64,1536]{2,1,0:T(8,128)(2,1)S(1)}, u32[]{:S(2)}, u32[]{:S(2)}) collective-permute-start(bf16[4,64,1536]{2,1,0:T(8,128)(2,1)S(1)} %bitcast.3), channel_id=1, source_target_pairs={{0,1},{1,0},{2,3},{3,2},{4,5},{5,4},{6,7},{7,6},{8,9},{9,8},{10,11... | collective-permute-start | bytes 2359304 | tf_op jit(solution)/shard_map/ppermute | solution.py:30
  40.8 18.3 %collective-permute-start.2 = (bf16[768,384]{1,0:T(8,128)(2,1)S(1)}, bf16[768,384]{1,0:T(8,128)(2,1)S(1)}, u32[]{:S(2)}, u32[]{:S(2)}) collective-permute-start(bf16[768,384]{1,0:T(8,128)(2,1)S(1)} %constant_dynamic-update-slice_fusion.refs_2_), channel_id=1, source_target_pairs={{0,128},{128,0},{1,129},{129,1},{2,130},{130,2},{3,131},{131,3},{4... | collective-permute-start | bytes 1769480 | tf_op jit(solution)/shard_map/ppermute | solution.py:30
  61.7 5.0 %copy-start.6 = (bf16[128,768]{1,0:T(8,128)(2,1)S(1)}, bf16[128,768]{1,0:T(8,128)(2,1)}, u32[]{:S(2)}) copy-start(bf16[128,768]{1,0:T(8,128)(2,1)} %param.17) | copy-start | bytes 589828
  61.7 19.5 %all-to-all-start.1 = ((bf16[4,128,1152]{2,1,0:T(8,128)(2,1)}), bf16[4,128,1152]{2,1,0:T(8,128)(2,1)S(1)}, u32[]{:S(2)}, u32[]{:S(2)}) async-start(bf16[4,128,1152]{2,1,0:T(8,128)(2,1)} %project_more.1), calls=%async_computation.1 | async-start | bytes 2359296 | tf_op jit(solution)/shard_map/all_to_all | solution.py:34
  68.0 31.0 %collective-permute-start.4 = (bf16[896,768]{1,0:T(8,128)(2,1)S(1)}, bf16[896,768]{1,0:T(8,128)(2,1)}, u32[]{:S(2)}, u32[]{:S(2)}) collective-permute-start(bf16[896,768]{1,0:T(8,128)(2,1)S(1)} %constant_dynamic-update-slice_fusion.3.w_own), channel_id=1, source_target_pairs={{0,128},{128,0},{1,129},{129,1},{2,130},{130,2},{3,131},{131,3},{4... | collective-permute-start | bytes 4128776 | tf_op jit(solution)/shard_map/ppermute | solution.py:30
  70.2 12.1 %copy-start.7 = (f32[768]{0:T(1024)S(1)}, f32[768]{0:T(1024)}, u32[]{:S(2)}) copy-start(f32[768]{0:T(1024)} %param.16) | copy-start | bytes 9220
  84.2 15.8 %all-to-all-start.2 = ((bf16[4,128,896]{2,1,0:T(8,128)(2,1)}), bf16[4,128,896]{2,1,0:T(8,128)(2,1)S(1)}, u32[]{:S(2)}, u32[]{:S(2)}) async-start(bf16[4,128,896]{2,1,0:T(8,128)(2,1)} %broadcast_in_dim.2), calls=%async_computation.2 | async-start | bytes 1835008 | tf_op jit(solution)/shard_map/all_to_all | solution.py:34
  102.3 2.6 %collective-permute-start.5 = (bf16[4,64,1536]{2,1,0:T(8,128)(2,1)S(1)}, bf16[4,64,1536]{2,1,0:T(8,128)(2,1)S(1)}, u32[]{:S(2)}, u32[]{:S(2)}) collective-permute-start(bf16[4,64,1536]{2,1,0:T(8,128)(2,1)S(1)} %output_sent.1), channel_id=1, source_target_pairs={{0,1},{1,0},{2,3},{3,2},{4,5},{5,4},{6,7},{7,6},{8,9},{9,8},{10,11... | collective-permute-start | bytes 2359304 | tf_op jit(solution)/shard_map/ppermute | solution.py:30
  105.1 34.3 %copy-start.2 = (bf16[4,6144]{1,0:T(4,128)(2,1)S(1)}, bf16[4,6144]{1,0:T(4,128)(2,1)}, u32[]{:S(2)}) copy-start(bf16[4,6144]{1,0:T(4,128)(2,1)} %tokens.1) | copy-start | bytes 147460

commit v3 on v2

v3 whole, which is shorter than its diff:
```python
import functools
import math

import jax
import jax.numpy as jnp
from jax import lax
from jax.experimental import pallas as pl
from jax.experimental.pallas import tpu as pltpu
from jax.sharding import Mesh
from jax.sharding import PartitionSpec as P


HEAD = 128
DP = ("xl", "y")
MP = ("z", "xh", "c")
ALL = DP + MP
BF = jnp.bfloat16
F32 = jnp.float32
ANY = pl.BlockSpec(memory_space=pl.ANY)
VMEM = pl.BlockSpec(memory_space=pltpu.VMEM)


def normalize(values):
    center = values - jnp.mean(values, axis=-1, keepdims=True)
    spread = jnp.mean(center * center, axis=-1, keepdims=True)
    return center * lax.rsqrt(spread + 1e-06)


def partner(array, axis):
    return lax.ppermute(array, axis, [(0, 1), (1, 0)])


def exchange(pieces, axes):
    return lax.all_to_all(pieces, axes, split_axis=0, concat_axis=0, tiled=True)


def dot(a, b):
    return lax.dot_general(a, b, (((a.ndim - 1,), (0,)), ((), ())), preferred_element_type=F32)


def params(mib):
    return pltpu.CompilerParams(vmem_limit_bytes=mib * 1024 * 1024)


def cost(flops, moved):
    return pl.CostEstimate(flops=flops, bytes_accessed=moved, transcendentals=0)


def spread_kernel(n_y, n_z, tokens, received, norm_gain, out, own, beside, gain, sems):
    _, width = own.shape
    cols = width // (2 * n_y)
    copies = [
        pltpu.make_async_copy(tokens, own, sems.at[0]),
        pltpu.make_async_copy(received, beside, sems.at[1]),
        pltpu.make_async_copy(norm_gain, gain, sems.at[2]),
    ]
    for copy in copies:
        copy.start()
    for copy in copies:
        copy.wait()
    mine, theirs = own[...].astype(F32), beside[...].astype(F32)
    first = lax.axis_index("xh") == 0
    rows = jnp.concatenate(
        (jnp.where(first, mine, theirs), jnp.where(first, theirs, mine)), axis=0
    )
    normed = normalize(rows) * gain[...]
    lower = lax.axis_index("xl") == 0
    for y in range(n_y):
        a = normed[:, y * cols : (y + 1) * cols]
        b = normed[:, (n_y + y) * cols : (n_y + y + 1) * cols]
        left = jnp.where(lower, a, b).astype(BF)
        right = jnp.where(lower, b, a).astype(BF)
        for z in range(n_z):
            out[y * n_z + z, :, :cols] = left
            out[y * n_z + z, :, cols:] = right


def spread(tokens, beside, gain, n_y, n_z):
    count, width = tokens.shape
    return pl.pallas_call(
        functools.partial(spread_kernel, n_y, n_z),
        out_shape=jax.ShapeDtypeStruct((n_y * n_z, 2 * count, width // n_y), BF),
        in_specs=[ANY] * 3,
        out_specs=VMEM,
        scratch_shapes=[
            pltpu.VMEM((count, width), BF),
            pltpu.VMEM((count, width), BF),
            pltpu.VMEM((1, width), F32),
            pltpu.SemaphoreType.DMA((3,)),
        ],
        compiler_params=pltpu.CompilerParams(vmem_limit_bytes=67_000_000),
        cost_estimate=cost(20 * count * width, 2 * 1024 * 1024),
        name="normed_pieces",
    )(tokens, beside, gain.reshape(1, width))


def product(rows, w, w_p, at):
    cols = rows.shape[1] // 2
    return dot(rows[:, :cols], w[:, at]) + dot(rows[:, cols:], w_p[:, at])


def inner_kernel(tokens, w_own, w_other, out, rows, kept, kept_p, sems):
    copies = [
        pltpu.make_async_copy(tokens, rows, sems.at[0]),
        pltpu.make_async_copy(w_own, kept, sems.at[1]),
        pltpu.make_async_copy(w_other, kept_p, sems.at[2]),
    ]
    for copy in copies:
        copy.start()
    for copy in copies:
        copy.wait()
    images, half, width = rows.shape
    left = rows[...].reshape(images * half, width)
    for n in range(kept.shape[1] // 384):
        at = slice(n * 384, (n + 1) * 384)
        value = product(left, kept, kept_p, at)
        out[:, :, at] = value.astype(BF).reshape(images, half, 384)


def inner_part(tokens, w_own, w_other):
    images, half, width = tokens.shape
    columns = w_own.shape[1]
    return pl.pallas_call(
        inner_kernel,
        out_shape=jax.ShapeDtypeStruct((images, half, columns), BF),
        in_specs=[ANY, ANY, ANY],
        out_specs=VMEM,
        scratch_shapes=[
            pltpu.VMEM(tokens.shape, BF),
            pltpu.VMEM(w_own.shape, BF),
            pltpu.VMEM(w_other.shape, BF),
            pltpu.SemaphoreType.DMA((3,)),
        ],
        compiler_params=params(12),
        cost_estimate=cost(2 * images * half * width * columns, 4 * 1024 * 1024),
        name="inner_part",
    )(tokens, w_own, w_other)


def heads_kernel(
    mine, theirs, w_own, w_other, inner_mine, inner_theirs, out, rows, rows_p, kept, kept_p, sems
):
    images, half, width = rows.shape
    wide = w_own.shape[1]
    copies = [
        pltpu.make_async_copy(mine, rows, sems.at[0]),
        pltpu.make_async_copy(w_own, kept, sems.at[1]),
        pltpu.make_async_copy(w_other, kept_p, sems.at[2]),
        pltpu.make_async_copy(theirs, rows_p, sems.at[3]),
        pltpu.make_async_copy(inner_mine, out.at[:, :half, wide:], sems.at[4]),
        pltpu.make_async_copy(inner_theirs, out.at[:, half:, wide:], sems.at[5]),
    ]
    for copy in copies:
        copy.start()
    for copy in copies[:3]:
        copy.wait()
    for part, source in enumerate((rows, rows_p)):
        if part:
            copies[3].wait()
        left = source[...].reshape(images * half, width)
        value = product(left, kept, kept_p, slice(0, wide))
        out[:, part * half : (part + 1) * half, :wide] = value.astype(BF).reshape(
            images, half, wide
        )
    for copy in copies[4:]:
        copy.wait()


def heads_part(mine, theirs, w_own, w_other, inner_mine, inner_theirs):
    images, half, width = mine.shape
    wide = w_own.shape[1]
    return pl.pallas_call(
        heads_kernel,
        out_shape=jax.ShapeDtypeStruct((images, 2 * half, wide + inner_mine.shape[2]), BF),
        in_specs=[ANY, ANY, ANY, ANY, ANY, ANY],
        out_specs=VMEM,
        scratch_shapes=[pltpu.VMEM(mine.shape, BF)] * 2
        + [pltpu.VMEM(w_own.shape, BF)] * 2
        + [pltpu.SemaphoreType.DMA((6,))],
        compiler_params=params(12),
        cost_estimate=cost(4 * images * half * width * wide, 4 * 1024 * 1024),
        name="heads_part",
    )(mine, theirs, w_own, w_other, inner_mine, inner_theirs)


def middle_kernel(arrived, bias, scale, out, kept, sem):
    copy = pltpu.make_async_copy(bias, kept, sem)
    copy.start()
    copies, columns = out.shape[0], kept.shape[0]

    def summed(at):
        total = arrived[0, :, at].astype(F32)
        for n in range(1, arrived.shape[0]):
            total = total + arrived[n, :, at].astype(F32)
        return total

    def rounded(n):
        return summed(slice(n * HEAD, (n + 1) * HEAD)).astype(BF)

    query_norm = normalize(rounded(0).astype(F32)).astype(BF)
    key_norm = normalize(rounded(1).astype(F32)).astype(BF)
    scores = lax.dot_general(
        query_norm, key_norm, (((1,), (1,)), ((), ())), preferred_element_type=F32
    )
    scores = scores * scale[0]
    powers = jnp.exp(scores - jnp.max(scores, axis=-1, keepdims=True))
    probs = (powers / jnp.sum(powers, axis=-1, keepdims=True)).astype(BF)
    mixed = dot(probs, rounded(2)).astype(BF)
    for n in range(copies):
        out[n, :, :HEAD] = mixed
    copy.wait()
    for m in range(columns // 256):
        at = slice(m * 256, (m + 1) * 256)
        inner = summed(slice(3 * HEAD + m * 256, 3 * HEAD + (m + 1) * 256)) + kept[at]
        activ = (inner * (0.5 + 0.5 * lax.erf(inner * math.sqrt(0.5)))).astype(BF)
        for n in range(copies):
            out[n, :, HEAD + m * 256 : HEAD + (m + 1) * 256] = activ


def middle(arrived, bias, scale):
    copies, patches, _ = arrived.shape
    columns = bias.shape[0]
    return pl.pallas_call(
        middle_kernel,
        out_shape=jax.ShapeDtypeStruct((copies, patches, HEAD + columns), BF),
        in_specs=[VMEM, ANY, pl.BlockSpec(memory_space=pltpu.SMEM)],
        out_specs=VMEM,
        scratch_shapes=[pltpu.VMEM((columns,), F32), pltpu.SemaphoreType.DMA],
        compiler_params=params(12),
        cost_estimate=cost(60 * patches * columns, 2 * 1024 * 1024),
        name="middle",
    )(arrived, bias, scale)


def output_kernel(part, features, *refs):
    sources, out, rows, kept, sems = refs[:4], refs[4], refs[5], refs[6:8], refs[8]
    images, half, width = rows.shape
    heads = sources[0].shape[0]
    cols = kept[0].shape[1]
    first = pltpu.make_async_copy(
        features.at[:, part * half : (part + 1) * half], rows, sems.at[4]
    )
    copies = []
    for n, source in enumerate(sources):
        to = kept[n // 2].at[pl.ds(heads, width - heads) if n % 2 else pl.ds(0, heads)]
        copies.append(pltpu.make_async_copy(source, to, sems.at[n]))
    first.start()
    for copy in copies:
        copy.start()
    first.wait()
    left = rows[...].reshape(images * half, width)
    for n in range(2):
        copies[2 * n].wait()
        copies[2 * n + 1].wait()
        for m in range(2):
            at = slice(m * cols // 2, (m + 1) * cols // 2)
            value = dot(left, kept[n][:, at]).astype(out.dtype)
            to = slice(n * cols + m * cols // 2, n * cols + (m + 1) * cols // 2)
            out[:, :, to] = value.reshape(images, half, cols // 2)


def output(features, weights, part, kind):
    images, patches, width = features.shape
    half, cols = patches // 2, weights[0].shape[1]
    return pl.pallas_call(
        functools.partial(output_kernel, part),
        out_shape=jax.ShapeDtypeStruct((images, half, 2 * cols), kind),
        in_specs=[ANY] * 5,
        out_specs=VMEM,
        scratch_shapes=[pltpu.VMEM((images, half, width), BF)]
        + [pltpu.VMEM((width, cols), BF)] * 2
        + [pltpu.SemaphoreType.DMA((5,))],
        compiler_params=params(16),
        cost_estimate=cost(4 * images * half * width * cols, 4 * 1024 * 1024),
        name="output_sent" if part else "output_kept",
    )(features, *weights)


def finish_kernel(n_y, arrived, tokens, out):
    pieces, _, width = arrived.shape
    cols = width // 2
    lower = lax.axis_index("xl") == 0
    for y in range(n_y):
        at = slice(y * pieces // n_y, (y + 1) * pieces // n_y)
        total = arrived[at].astype(F32).sum(axis=0)
        left, right = total[:, :cols], total[:, cols:]
        for n, value in enumerate(
            (jnp.where(lower, left, right), jnp.where(lower, right, left))
        ):
            to = slice((n * n_y + y) * cols, (n * n_y + y + 1) * cols)
            out[:, to] = (tokens[:, to].astype(F32) + value).astype(BF)


def finish(arrived, tokens, n_y):
    return pl.pallas_call(
        functools.partial(finish_kernel, n_y),
        out_shape=jax.ShapeDtypeStruct(tokens.shape, BF),
        in_specs=[VMEM] * 2,
        out_specs=VMEM,
        compiler_params=params(8),
        cost_estimate=cost(arrived.size, 2 * 1024 * 1024),
        name="finish",
    )(arrived, tokens)


def block(
    tokens, norm_gain, w_query, w_key, w_value, w_inner, bias_inner, w_attn_out, w_outer, temper
):
    count = tokens.shape[0]
    n_y, n_z, n_xh = (lax.axis_size(a) for a in ("y", "z", "xh"))
    beside = partner(tokens, "xh")
    w_qkv = jnp.concatenate((w_query, w_key, w_value), axis=1)
    w_inner_p = partner(w_inner, "xl")
    w_qkv_p = partner(w_qkv, "xl")
    w_attn_out_p = partner(w_attn_out, "xl")
    w_outer_p = partner(w_outer, "xl")
    pieces = spread(tokens, beside, norm_gain, n_y, n_z)
    mine = exchange(pieces, ("y", "z"))
    mine = mine.reshape(n_y, -1, mine.shape[-1])
    theirs = partner(mine, "c")
    inner_mine = inner_part(mine, w_inner, w_inner_p)
    inner_theirs = inner_part(theirs, w_inner, w_inner_p)
    partial = heads_part(mine, theirs, w_qkv, w_qkv_p, inner_mine, inner_theirs)
    arrived = exchange(partial, "y")
    scale = temper / math.sqrt(HEAD)
    features = middle(arrived, bias_inner, scale)
    features, w_attn_out_p, w_outer_p = lax.optimization_barrier(
        (features, w_attn_out_p, w_outer_p)
    )
    w_out = (w_attn_out, w_outer, w_attn_out_p, w_outer_p)
    features = exchange(features, "y")
    sent = partner(output(features, w_out, 1, BF), "c")
    kept = output(features, w_out, 0, F32)
    summed = (kept + sent.astype(F32)).astype(BF)
    pieces = summed.reshape(n_y * n_z * n_xh, count, summed.shape[-1])
    arrived = exchange(pieces, ("y", "z", "xh"))
    return finish(arrived, tokens, n_y)


def solution(mesh):
    finer = Mesh(mesh.devices.reshape(2, 4, 8, 2, 2), ALL)
    return jax.shard_map(
        block,
        mesh=finer,
        in_specs=(
            P(ALL, None),
            P(),
            P(DP, MP),
            P(DP, MP),
            P(DP, MP),
            P(DP, MP),
            P(MP),
            P(MP, DP),
            P(MP, DP),
            P(MP),
        ),
        out_specs=P(ALL, None),
        check_vma=False,
    )
```

time: 141 us -> 147 us (1.043)
  blocking collectives: 34.1 us -> 50.8 us
  starting transfers between devices: 29.6 us -> 25.1 us
  local copies, waits for them, and re-layouts: 5.29 us -> 1.28 us
  waiting for transfers between devices: 56.4 us -> 52.6 us
  Pallas kernels: 12 us -> 15.6 us
    all_to_all x1 -> x2, blocking collectives: 34.1 us -> 50.8 us  [exchange(): return lax.all_to_all(pieces, axes, split_axis=0, concat_axis=0, tiled=True)]
    all_to_all x3 -> x2, starting transfers between devices: 21.6 us -> 16.8 us  [exchange(): return lax.all_to_all(pieces, axes, split_axis=0, concat_axis=0, tiled=True)]
    all_to_all x3 -> x2, waiting for transfers between devices: 29.7 us -> 27.7 us  [exchange(): return lax.all_to_all(pieces, axes, split_axis=0, concat_axis=0, tiled=True)]
    ppermute x6 -> x7, waiting for transfers between devices: 26.7 us -> 24.9 us  [partner(): return lax.ppermute(array, axis, [(0, 1), (1, 0)])]
    unnamed x19 -> x14, local copies, waits for them, and re-layouts: 1.66 us -> 0.12 us
    pallas_call x2 -> x4, Pallas kernels: 5.23 us -> 6.58 us  [the longest x2 3.08 us: inner_part(): pl.pallas_call(inner_kernel, out_shape=jax.ShapeDtypeStruct((images, half...]
    ppermute x6 -> x7, starting transfers between devices: 8.04 us -> 8.3 us  [partner(): return lax.ppermute(array, axis, [(0, 1), (1, 0)])]
  transfers between devices with their start and end apart: 9 -> 9, of which waited for: 7 -> 6; matrix products, arithmetic and copies ran while one was open for 4% -> 1% of each run, Pallas kernels for 3% -> 7%
where the time goes in v3:
time: 147 us; the launch traced here: 146 us
  waiting for transfers between devices  52.6 us (36%)
  blocking collectives  50.8 us (35%)
  starting transfers between devices  25.1 us (17%)
  Pallas kernels  15.6 us (11%)
    all_to_all x2, blocking collectives, exchange(): return lax.all_to_all(pieces, axes, split_axis=0, concat_axis=0, tiled=True)  50.8 us
    all_to_all x2, waiting for transfers between devices, exchange(): return lax.all_to_all(pieces, axes, split_axis=0, concat_axis=0, tiled=True)  27.7 us
    ppermute x7, waiting for transfers between devices, partner(): return lax.ppermute(array, axis, [(0, 1), (1, 0)])  24.9 us
    all_to_all x2, starting transfers between devices, exchange(): return lax.all_to_all(pieces, axes, split_axis=0, concat_axis=0, tiled=True)  16.8 us
    ppermute x7, starting transfers between devices, partner(): return lax.ppermute(array, axis, [(0, 1), (1, 0)])  8.3 us
    pallas_call x2, Pallas kernels, output(): pl.pallas_call(functools.partial(output_kernel, part), out_shape=jax.Shap...  6 us
    pallas_call x2, Pallas kernels, inner_part(): pl.pallas_call(inner_kernel, out_shape=jax.ShapeDtypeStruct((images, half...  3.08 us
  transfers between devices with their start and end apart: 9, of which 6 were waited for; matrix products, arithmetic and copies ran while one was open for 1% of the time, Pallas kernels for 7%

profile of v3, /device:TPU:8, one launch (start us, length us, event | category | flops | bytes accessed | tf_op | source)
XLA Modules:
  0.0 146.4 jit_solution(3227126955324887575)
XLA Ops:
  0.0 3.0 %collective-permute-start = (bf16[4,6144]{1,0:T(4,128)(2,1)}, bf16[4,6144]{1,0:T(4,128)(2,1)}, u32[]{:S(2)}, u32[]{:S(2)}) collective-permute-start(bf16[4,6144]{1,0:T(4,128)(2,1)} %tokens.3), channel_id=1, source_target_pairs={{0,2},{2,0},{1,3},{3,1},{4,6},{6,4},{5,7},{7,5},{8,10},{10,8},{9,1... | collective-permute-start | bytes 147464 | tf_op jit(solution)/shard_map/ppermute | solution.py:30
  3.0 2.9 %collective-permute-done.received = bf16[4,6144]{1,0:T(4,128)(2,1)} collective-permute-done((bf16[4,6144]{1,0:T(4,128)(2,1)}, bf16[4,6144]{1,0:T(4,128)(2,1)}, u32[]{:S(2)}, u32[]{:S(2)}) %collective-permute-start) | collective-permute-done | bytes 49184 | tf_op jit(solution)/shard_map/ppermute | solution.py:30
  5.9 2.1 %normed_pieces.1 = bf16[32,8,1536]{2,1,0:T(8,128)(2,1)} custom-call(bf16[4,6144]{1,0:T(4,128)(2,1)} %tokens.3, bf16[4,6144]{1,0:T(4,128)(2,1)} %collective-permute-done.received, f32[1,6144]{1,0:T(1,128)} %bitcast.5), custom_call_target="tpu_custom_call" | custom-call | flops 491520 | bytes 2097152 | tf_op jit(solution)/shard_map/normed_pieces/pallas_call | solution.py:80
  8.0 0.0 copy-start
  8.0 0.0 copy-start.4
  8.0 0.0 copy-start.5
  8.0 11.8 %all-to-all-start = ((bf16[32,8,1536]{2,1,0:T(8,128)(2,1)}), bf16[32,8,1536]{2,1,0:T(8,128)(2,1)S(1)}, u32[]{:S(2)}, u32[]{:S(2)}) async-start(bf16[32,8,1536]{2,1,0:T(8,128)(2,1)} %normed_pieces.1), calls=%async_computation | async-start | bytes 1572864 | tf_op jit(solution)/shard_map/all_to_all | solution.py:34
  19.9 0.0 copy-done
  19.9 1.6 %collective-permute-start.3 = (bf16[768,768]{1,0:T(8,128)(2,1)S(1)}, bf16[768,768]{1,0:T(8,128)(2,1)S(1)}, u32[]{:S(2)}, u32[]{:S(2)}) collective-permute-start(bf16[768,768]{1,0:T(8,128)(2,1)S(1)} %copy-done), channel_id=1, source_target_pairs={{0,128},{128,0},{1,129},{129,1},{2,130},{130,2},{3,131},{131,3},{4... | collective-permute-start | bytes 3538952 | tf_op jit(solution)/shard_map/ppermute | solution.py:30
  21.5 17.8 %all-to-all-done = bf16[32,8,1536]{2,1,0:T(8,128)(2,1)S(1)} async-done(((bf16[32,8,1536]{2,1,0:T(8,128)(2,1)}), bf16[32,8,1536]{2,1,0:T(8,128)(2,1)S(1)}, u32[]{:S(2)}, u32[]{:S(2)}) %all-to-all-start) | async-done | bytes 786464 | tf_op jit(solution)/shard_map/all_to_all | solution.py:34
  39.3 0.0 collective-permute-start.1
  39.3 0.0 copy-done.4
  39.3 0.0 copy-done.5
  39.4 1.0 constant_dynamic-update-slice_fusion.w_own
  40.4 1.6 %collective-permute-start.2 = (bf16[768,384]{1,0:T(8,128)(2,1)S(1)}, bf16[768,384]{1,0:T(8,128)(2,1)S(1)}, u32[]{:S(2)}, u32[]{:S(2)}) collective-permute-start(bf16[768,384]{1,0:T(8,128)(2,1)S(1)} %constant_dynamic-update-slice_fusion.w_own), channel_id=1, source_target_pairs={{0,128},{128,0},{1,129},{129,1},{2,130},{130,2},{3,131},{131,3},{4... | collective-permute-start | bytes 1769480 | tf_op jit(solution)/shard_map/ppermute | solution.py:30
  41.9 0.5 collective-permute-start.5
  42.5 6.0 %collective-permute-done.3.w_other = bf16[768,768]{1,0:T(8,128)(2,1)S(1)} collective-permute-done((bf16[768,768]{1,0:T(8,128)(2,1)S(1)}, bf16[768,768]{1,0:T(8,128)(2,1)S(1)}, u32[]{:S(2)}, u32[]{:S(2)}) %collective-permute-start.3) | collective-permute-done | bytes 1179680 | tf_op jit(solution)/shard_map/ppermute | solution.py:30
  48.4 1.5 %inner_part.2.inner_mine = bf16[4,64,768]{2,1,0:T(8,128)(2,1)S(1)} custom-call(bf16[4,64,1536]{2,1,0:T(8,128)(2,1)S(1)} %bitcast.3, bf16[768,768]{1,0:T(8,128)(2,1)S(1)} %copy-done, bf16[768,768]{1,0:T(8,128)(2,1)S(1)} %collective-permute-done.3.w_other), custom_call_target="tpu_custom_call" | custom-call | flops 603979776 | bytes 4194304 | tf_op jit(solution)/shard_map/inner_part/pallas_call | solution.py:123
  50.0 0.0 collective-permute-done.1.tokens.theirs
  50.0 1.5 %inner_part.3.inner_theirs = bf16[4,64,768]{2,1,0:T(8,128)(2,1)S(1)} custom-call(bf16[4,64,1536]{2,1,0:T(8,128)(2,1)S(1)} %collective-permute-done.1.tokens.theirs, bf16[768,768]{1,0:T(8,128)(2,1)S(1)} %copy-done, bf16[768,768]{1,0:T(8,128)(2,1)S(1)} %collective-permute-done.3.w_other), custom_call_target="tpu_custom_call" | custom-call | flops 603979776 | bytes 4194304 | tf_op jit(solution)/shard_map/inner_part/pallas_call | solution.py:123
  51.5 9.5 %collective-permute-done.2.w_other = bf16[768,384]{1,0:T(8,128)(2,1)S(1)} collective-permute-done((bf16[768,384]{1,0:T(8,128)(2,1)S(1)}, bf16[768,384]{1,0:T(8,128)(2,1)S(1)}, u32[]{:S(2)}, u32[]{:S(2)}) %collective-permute-start.2) | collective-permute-done | bytes 589856 | tf_op jit(solution)/shard_map/ppermute | solution.py:30
  61.1 2.6 %heads_part.1 = bf16[4,128,1152]{2,1,0:T(8,128)(2,1)} custom-call(bf16[4,64,1536]{2,1,0:T(8,128)(2,1)S(1)} %bitcast.4, bf16[4,64,1536]{2,1,0:T(8,128)(2,1)S(1)} %collective-permute-done.1.tokens.theirs, bf16[768,384]{1,0:T(8,128)(2,1)S(1)} %constant_dynamic-update-slice_fusion.w_own, bf16[768,384]{1,0:T(8,128)(2,1)S(1)} %collective-permute-done.2.w_other, ...), custom_call_target="tpu_custom_call" | custom-call | flops 603979776 | bytes 4194304 | tf_op jit(solution)/shard_map/heads_part/pallas_call | solution.py:172
  63.7 0.0 copy-start.1
  63.7 0.0 copy-start.3
  63.8 5.0 %all-to-all-start.1 = ((bf16[4,128,1152]{2,1,0:T(8,128)(2,1)}), bf16[4,128,1152]{2,1,0:T(8,128)(2,1)S(1)}, u32[]{:S(2)}, u32[]{:S(2)}) async-start(bf16[4,128,1152]{2,1,0:T(8,128)(2,1)} %heads_part.1), calls=%async_computation.1 | async-start | bytes 2359296 | tf_op jit(solution)/shard_map/all_to_all | solution.py:34
  68.7 0.0 copy-done.1
  68.7 1.5 %collective-permute-start.4 = (bf16[128,768]{1,0:T(8,128)(2,1)S(1)}, bf16[128,768]{1,0:T(8,128)(2,1)S(1)}, u32[]{:S(2)}, u32[]{:S(2)}) collective-permute-start(bf16[128,768]{1,0:T(8,128)(2,1)S(1)} %copy-done.1), channel_id=1, source_target_pairs={{0,128},{128,0},{1,129},{129,1},{2,130},{130,2},{3,131},{131,3},{4... | collective-permute-start | bytes 589832 | tf_op jit(solution)/shard_map/ppermute | solution.py:30
  70.9 9.9 %all-to-all-done.1.arrived = bf16[4,128,1152]{2,1,0:T(8,128)(2,1)S(1)} async-done(((bf16[4,128,1152]{2,1,0:T(8,128)(2,1)}), bf16[4,128,1152]{2,1,0:T(8,128)(2,1)S(1)}, u32[]{:S(2)}, u32[]{:S(2)}) %all-to-all-start.1) | async-done | bytes 1179680 | tf_op jit(solution)/shard_map/all_to_all | solution.py:34
  80.8 0.0 copy-done.3
  80.8 0.9 middle.1
  81.7 6.5 %collective-permute-done.4.refs_2_ = bf16[128,768]{1,0:T(8,128)(2,1)S(1)} collective-permute-done((bf16[128,768]{1,0:T(8,128)(2,1)S(1)}, bf16[128,768]{1,0:T(8,128)(2,1)S(1)}, u32[]{:S(2)}, u32[]{:S(2)}) %collective-permute-start.4) | collective-permute-done | bytes 196640 | tf_op jit(solution)/shard_map/ppermute | solution.py:30
  88.1 0.0 collective-permute-done.5.refs_3_
  88.1 15.4 %all_to_all.20.features = bf16[4,128,896]{2,1,0:T(8,128)(2,1)S(1)} all-to-all(bf16[4,128,896]{2,1,0:T(8,128)(2,1)S(1)} %middle.1), channel_id=1, replica_groups=mesh['xl'=2,'y'=4,'z'=8,'xh'=2,'c'=2] {'y'}, dimensions={0} | all-to-all | bytes 1835008 | tf_op jit(solution)/shard_map/all_to_all | solution.py:34
  103.6 3.0 %output_sent.1 = bf16[4,64,1536]{2,1,0:T(8,128)(2,1)S(1)} custom-call(bf16[4,128,896]{2,1,0:T(8,128)(2,1)S(1)} %all_to_all.20.features, bf16[128,768]{1,0:T(8,128)(2,1)S(1)} %copy-done.1, bf16[768,768]{1,0:T(8,128)(2,1)} %refs_1_.3, bf16[128,768]{1,0:T(8,128)(2,1)S(1)} %collective-permute-done.4.refs_2_, bf16[768,768]{1,0:T(8,128)(2,1)} %collective-permute-done.5.refs_3_), custom_call_target="tpu_custom_call" | custom-call | flops 704643072 | bytes 4194304 | tf_op jit(solution)/shard_map/output_sent/pallas_call | solution.py:265
  106.6 0.1 collective-permute-start.6
  106.7 3.0 %output_kept.1 = f32[4,64,1536]{2,1,0:T(8,128)S(1)} custom-call(bf16[4,128,896]{2,1,0:T(8,128)(2,1)S(1)} %all_to_all.20.features, bf16[128,768]{1,0:T(8,128)(2,1)S(1)} %copy-done.1, bf16[768,768]{1,0:T(8,128)(2,1)} %refs_1_.3, bf16[128,768]{1,0:T(8,128)(2,1)S(1)} %collective-permute-done.4.refs_2_, bf16[768,768]{1,0:T(8,128)(2,1)} %collective-permute-done.5.refs_3_), custom_call_target="tpu_custom_call" | custom-call | flops 704643072 | bytes 4194304 | tf_op jit(solution)/shard_map/output_kept/pallas_call | solution.py:265
  109.7 0.0 collective-permute-done.6
  109.7 0.2 add_convert_fusion
  109.9 0.2 reshape.11
  110.1 0.0 copy-start.2
  110.1 35.3 %all_to_all.21.arrived = bf16[64,4,1536]{2,1,0:T(4,128)(2,1)S(1)} all-to-all(bf16[64,4,1536]{2,1,0:T(4,128)(2,1)S(1)} %reshape.11), channel_id=1, replica_groups=mesh['xl'=2,'y'=4,'z'=8,'xh'=2,'c'=2] {'y','z','xh'}, dimensions={0} | all-to-all | bytes 1572864 | tf_op jit(solution)/shard_map/all_to_all | solution.py:34
  145.4 0.0 copy-done.2
  145.4 1.0 finish.1
  (2 shorter events, 0.1 us)
Async XLA Ops:
  0.0 5.9 %collective-permute-start = (bf16[4,6144]{1,0:T(4,128)(2,1)}, bf16[4,6144]{1,0:T(4,128)(2,1)}, u32[]{:S(2)}, u32[]{:S(2)}) collective-permute-start(bf16[4,6144]{1,0:T(4,128)(2,1)} %tokens.3), channel_id=1, source_target_pairs={{0,2},{2,0},{1,3},{3,1},{4,6},{6,4},{5,7},{7,5},{8,10},{10,8},{9,1... | collective-permute-start | bytes 147464 | tf_op jit(solution)/shard_map/ppermute | solution.py:30
  8.0 11.9 %copy-start = (bf16[768,768]{1,0:T(8,128)(2,1)S(1)}, bf16[768,768]{1,0:T(8,128)(2,1)}, u32[]{:S(2)}) copy-start(bf16[768,768]{1,0:T(8,128)(2,1)} %w_own.3) | copy-start | bytes 3538948
  8.0 31.3 %copy-start.4 = (bf16[768,128]{1,0:T(8,128)(2,1)S(1)}, bf16[768,128]{1,0:T(8,128)(2,1)}, u32[]{:S(2)}) copy-start(bf16[768,128]{1,0:T(8,128)(2,1)} %param.12) | copy-start | bytes 589828
  8.0 31.3 %copy-start.5 = (bf16[768,128]{1,0:T(8,128)(2,1)S(1)}, bf16[768,128]{1,0:T(8,128)(2,1)}, u32[]{:S(2)}) copy-start(bf16[768,128]{1,0:T(8,128)(2,1)} %param.13) | copy-start | bytes 589828
  8.0 31.2 %all-to-all-start = ((bf16[32,8,1536]{2,1,0:T(8,128)(2,1)}), bf16[32,8,1536]{2,1,0:T(8,128)(2,1)S(1)}, u32[]{:S(2)}, u32[]{:S(2)}) async-start(bf16[32,8,1536]{2,1,0:T(8,128)(2,1)} %normed_pieces.1), calls=%async_computation | async-start | bytes 1572864 | tf_op jit(solution)/shard_map/all_to_all | solution.py:34
  19.9 28.5 %collective-permute-start.3 = (bf16[768,768]{1,0:T(8,128)(2,1)S(1)}, bf16[768,768]{1,0:T(8,128)(2,1)S(1)}, u32[]{:S(2)}, u32[]{:S(2)}) collective-permute-start(bf16[768,768]{1,0:T(8,128)(2,1)S(1)} %copy-done), channel_id=1, source_target_pairs={{0,128},{128,0},{1,129},{129,1},{2,130},{130,2},{3,131},{131,3},{4... | collective-permute-start | bytes 3538952 | tf_op jit(solution)/shard_map/ppermute | solution.py:30
  39.3 10.7 %collective-permute-start.1 = (bf16[4,64,1536]{2,1,0:T(8,128)(2,1)S(1)}, bf16[4,64,1536]{2,1,0:T(8,128)(2,1)S(1)}, u32[]{:S(2)}, u32[]{:S(2)}) collective-permute-start(bf16[4,64,1536]{2,1,0:T(8,128)(2,1)S(1)} %bitcast.2), channel_id=1, source_target_pairs={{0,1},{1,0},{2,3},{3,2},{4,5},{5,4},{6,7},{7,6},{8,9},{9,8},{10,11... | collective-permute-start | bytes 2359304 | tf_op jit(solution)/shard_map/ppermute | solution.py:30
  40.4 20.7 %collective-permute-start.2 = (bf16[768,384]{1,0:T(8,128)(2,1)S(1)}, bf16[768,384]{1,0:T(8,128)(2,1)S(1)}, u32[]{:S(2)}, u32[]{:S(2)}) collective-permute-start(bf16[768,384]{1,0:T(8,128)(2,1)S(1)} %constant_dynamic-update-slice_fusion.w_own), channel_id=1, source_target_pairs={{0,128},{128,0},{1,129},{129,1},{2,130},{130,2},{3,131},{131,3},{4... | collective-permute-start | bytes 1769480 | tf_op jit(solution)/shard_map/ppermute | solution.py:30
  41.9 46.2 %collective-permute-start.5 = (bf16[768,768]{1,0:T(8,128)(2,1)}, bf16[768,768]{1,0:T(8,128)(2,1)}, u32[]{:S(2)}, u32[]{:S(2)}) collective-permute-start(bf16[768,768]{1,0:T(8,128)(2,1)} %refs_1_.3), channel_id=1, source_target_pairs={{0,128},{128,0},{1,129},{129,1},{2,130},{130,2},{3,131},{131,3},{4... | collective-permute-start | bytes 3538952 | tf_op jit(solution)/shard_map/ppermute | solution.py:30
  63.7 5.0 %copy-start.1 = (bf16[128,768]{1,0:T(8,128)(2,1)S(1)}, bf16[128,768]{1,0:T(8,128)(2,1)}, u32[]{:S(2)}) copy-start(bf16[128,768]{1,0:T(8,128)(2,1)} %refs_0_.3) | copy-start | bytes 589828
  63.7 17.1 %copy-start.3 = (f32[768]{0:T(1024)S(1)}, f32[768]{0:T(1024)}, u32[]{:S(2)}) copy-start(f32[768]{0:T(1024)} %bias.1) | copy-start | bytes 9220
  63.8 17.0 %all-to-all-start.1 = ((bf16[4,128,1152]{2,1,0:T(8,128)(2,1)}), bf16[4,128,1152]{2,1,0:T(8,128)(2,1)S(1)}, u32[]{:S(2)}, u32[]{:S(2)}) async-start(bf16[4,128,1152]{2,1,0:T(8,128)(2,1)} %heads_part.1), calls=%async_computation.1 | async-start | bytes 2359296 | tf_op jit(solution)/shard_map/all_to_all | solution.py:34
  68.7 19.4 %collective-permute-start.4 = (bf16[128,768]{1,0:T(8,128)(2,1)S(1)}, bf16[128,768]{1,0:T(8,128)(2,1)S(1)}, u32[]{:S(2)}, u32[]{:S(2)}) collective-permute-start(bf16[128,768]{1,0:T(8,128)(2,1)S(1)} %copy-done.1), channel_id=1, source_target_pairs={{0,128},{128,0},{1,129},{129,1},{2,130},{130,2},{3,131},{131,3},{4... | collective-permute-start | bytes 589832 | tf_op jit(solution)/shard_map/ppermute | solution.py:30
  106.6 3.1 %collective-permute-start.6 = (bf16[4,64,1536]{2,1,0:T(8,128)(2,1)S(1)}, bf16[4,64,1536]{2,1,0:T(8,128)(2,1)S(1)}, u32[]{:S(2)}, u32[]{:S(2)}) collective-permute-start(bf16[4,64,1536]{2,1,0:T(8,128)(2,1)S(1)} %output_sent.1), channel_id=1, source_target_pairs={{0,1},{1,0},{2,3},{3,2},{4,5},{5,4},{6,7},{7,6},{8,9},{9,8},{10,11... | collective-permute-start | bytes 2359304 | tf_op jit(solution)/shard_map/ppermute | solution.py:30
  110.1 35.3 %copy-start.2 = (bf16[4,6144]{1,0:T(4,128)(2,1)S(1)}, bf16[4,6144]{1,0:T(4,128)(2,1)}, u32[]{:S(2)}) copy-start(bf16[4,6144]{1,0:T(4,128)(2,1)} %tokens.3) | copy-start | bytes 147460

commit v4 on v3

--- a/solution.py
+++ b/solution.py
@@ -218,11 +218,11 @@
 
 
 def middle(arrived, bias, scale):
-    copies, patches, _ = arrived.shape
+    _, patches, _ = arrived.shape
     columns = bias.shape[0]
     return pl.pallas_call(
         middle_kernel,
-        out_shape=jax.ShapeDtypeStruct((copies, patches, HEAD + columns), BF),
+        out_shape=jax.ShapeDtypeStruct((1, patches, HEAD + columns), BF),
         in_specs=[VMEM, ANY, pl.BlockSpec(memory_space=pltpu.SMEM)],
         out_specs=VMEM,
         scratch_shapes=[pltpu.VMEM((columns,), F32), pltpu.SemaphoreType.DMA],
@@ -232,48 +232,46 @@
     )(arrived, bias, scale)
 
 
-def output_kernel(part, features, *refs):
-    sources, out, rows, kept, sems = refs[:4], refs[4], refs[5], refs[6:8], refs[8]
+def output_kernel(part, features, w_own, w_other, out, rows, kept_own, kept_other, sems):
     images, half, width = rows.shape
-    heads = sources[0].shape[0]
-    cols = kept[0].shape[1]
-    first = pltpu.make_async_copy(
-        features.at[:, part * half : (part + 1) * half], rows, sems.at[4]
-    )
-    copies = []
-    for n, source in enumerate(sources):
-        to = kept[n // 2].at[pl.ds(heads, width - heads) if n % 2 else pl.ds(0, heads)]
-        copies.append(pltpu.make_async_copy(source, to, sems.at[n]))
-    first.start()
+    cols = kept_own.shape[1]
+    copies = [
+        pltpu.make_async_copy(
+            features.at[:, part * half : (part + 1) * half], rows, sems.at[0]
+        ),
+        pltpu.make_async_copy(w_own, kept_own, sems.at[1]),
+        pltpu.make_async_copy(w_other, kept_other, sems.at[2]),
+    ]
     for copy in copies:
         copy.start()
-    first.wait()
+    copies[0].wait()
     left = rows[...].reshape(images * half, width)
-    for n in range(2):
-        copies[2 * n].wait()
-        copies[2 * n + 1].wait()
+    for n, kept in enumerate((kept_own, kept_other)):
+        copies[n + 1].wait()
         for m in range(2):
             at = slice(m * cols // 2, (m + 1) * cols // 2)
-            value = dot(left, kept[n][:, at]).astype(out.dtype)
-            to = slice(n * cols + m * cols // 2, n * cols + (m + 1) * cols // 2)
-            out[:, :, to] = value.reshape(images, half, cols // 2)
-
-
-def output(features, weights, part, kind):
+            value = dot(left, kept[:, at]).astype(out.dtype).reshape(images, half, cols // 2)
+            out[:, :, n * cols + m * cols // 2 : n * cols + (m + 1) * cols // 2] = value
+
+
+def output(features, w_own, w_other, part, kind):
     images, patches, width = features.shape
-    half, cols = patches // 2, weights[0].shape[1]
+    half, cols = patches // 2, w_own.shape[1]
     return pl.pallas_call(
         functools.partial(output_kernel, part),
         out_shape=jax.ShapeDtypeStruct((images, half, 2 * cols), kind),
-        in_specs=[ANY] * 5,
-        out_specs=VMEM,
-        scratch_shapes=[pltpu.VMEM((images, half, width), BF)]
-        + [pltpu.VMEM((width, cols), BF)] * 2
-        + [pltpu.SemaphoreType.DMA((5,))],
+        in_specs=[ANY] * 3,
+        out_specs=VMEM,
+        scratch_shapes=[
+            pltpu.VMEM((images, half, width), BF),
+            pltpu.VMEM(w_own.shape, BF),
+            pltpu.VMEM(w_other.shape, BF),
+            pltpu.SemaphoreType.DMA((3,)),
+        ],
         compiler_params=params(16),
         cost_estimate=cost(4 * images * half * width * cols, 4 * 1024 * 1024),
         name="output_sent" if part else "output_kept",
-    )(features, *weights)
+    )(features, w_own, w_other)
 
 
 def finish_kernel(n_y, arrived, tokens, out):
@@ -312,8 +310,8 @@
     w_qkv = jnp.concatenate((w_query, w_key, w_value), axis=1)
     w_inner_p = partner(w_inner, "xl")
     w_qkv_p = partner(w_qkv, "xl")
-    w_attn_out_p = partner(w_attn_out, "xl")
-    w_outer_p = partner(w_outer, "xl")
+    w_out = jnp.concatenate((w_attn_out, w_outer), axis=0)
+    w_out_p = partner(w_out, "xl")
     pieces = spread(tokens, beside, norm_gain, n_y, n_z)
     mine = exchange(pieces, ("y", "z"))
     mine = mine.reshape(n_y, -1, mine.shape[-1])
@@ -323,14 +321,10 @@
     partial = heads_part(mine, theirs, w_qkv, w_qkv_p, inner_mine, inner_theirs)
     arrived = exchange(partial, "y")
     scale = temper / math.sqrt(HEAD)
-    features = middle(arrived, bias_inner, scale)
-    features, w_attn_out_p, w_outer_p = lax.optimization_barrier(
-        (features, w_attn_out_p, w_outer_p)
-    )
-    w_out = (w_attn_out, w_outer, w_attn_out_p, w_outer_p)
-    features = exchange(features, "y")
-    sent = partner(output(features, w_out, 1, BF), "c")
-    kept = output(features, w_out, 0, F32)
+    features = middle(arrived, bias_inner, scale)[0]
+    features = lax.all_gather(features, "y", axis=0, tiled=False)
+    sent = partner(output(features, w_out, w_out_p, 1, BF), "c")
+    kept = output(features, w_out, w_out_p, 0, F32)
     summed = (kept + sent.astype(F32)).astype(BF)
     pieces = summed.reshape(n_y * n_z * n_xh, count, summed.shape[-1])
     arrived = exchange(pieces, ("y", "z", "xh"))

time: 147 us -> 138 us (0.939)
  waiting for transfers between devices: 52.6 us -> 45.6 us
  blocking collectives: 50.8 us -> 49 us
    all_to_all x2 -> x1, blocking collectives: 50.8 us -> 35.9 us  [exchange(): return lax.all_to_all(pieces, axes, split_axis=0, concat_axis=0, tiled=True)]
    all_gather x0 -> x1, blocking collectives: none -> 13.2 us  [block(): features = lax.all_gather(features, 'y', axis=0, tiled=False)]
    ppermute x7 -> x6, waiting for transfers between devices: 24.9 us -> 16.9 us  [partner(): return lax.ppermute(array, axis, [(0, 1), (1, 0)])]
    pallas_call x2, Pallas kernels: 6 us -> 3.67 us  [output(): pl.pallas_call(functools.partial(output_kernel, part), out_shape=jax.Shap...]
    pallas_call x2, Pallas kernels: 3.08 us -> 5.36 us  [inner_part(): pl.pallas_call(inner_kernel, out_shape=jax.ShapeDtypeStruct((images, half...]
    unnamed x14 -> x17, local copies, waits for them, and re-layouts: 0.12 us -> 2.07 us
    ppermute x7 -> x6, starting transfers between devices: 8.3 us -> 6.9 us  [partner(): return lax.ppermute(array, axis, [(0, 1), (1, 0)])]
  transfers between devices with their start and end apart: 9 -> 8, of which waited for: 6 -> 6; matrix products, arithmetic and copies ran while one was open for 1% -> 1% of each run, Pallas kernels for 7% -> 8%
where the time goes in v4:
time: 138 us
  blocking collectives  49 us (36%)
  waiting for transfers between devices  45.6 us (33%)
  starting transfers between devices  23.7 us (17%)
  Pallas kernels  15.8 us (11%)
  local copies, waits for them, and re-layouts  2.38 us (2%)
    all_to_all x1, blocking collectives, exchange(): return lax.all_to_all(pieces, axes, split_axis=0, concat_axis=0, tiled=True)  35.9 us
    all_to_all x2, waiting for transfers between devices, exchange(): return lax.all_to_all(pieces, axes, split_axis=0, concat_axis=0, tiled=True)  28.6 us
    ppermute x6, waiting for transfers between devices, partner(): return lax.ppermute(array, axis, [(0, 1), (1, 0)])  16.9 us
    all_to_all x2, starting transfers between devices, exchange(): return lax.all_to_all(pieces, axes, split_axis=0, concat_axis=0, tiled=True)  16.8 us
    all_gather x1, blocking collectives, block(): features = lax.all_gather(features, 'y', axis=0, tiled=False)  13.2 us
    ppermute x6, starting transfers between devices, partner(): return lax.ppermute(array, axis, [(0, 1), (1, 0)])  6.9 us
    pallas_call x2, Pallas kernels, inner_part(): pl.pallas_call(inner_kernel, out_shape=jax.ShapeDtypeStruct((images, half...  5.36 us
    pallas_call x2, Pallas kernels, output(): pl.pallas_call(functools.partial(output_kernel, part), out_shape=jax.Shap...  3.67 us
  transfers between devices with their start and end apart: 8, of which 6 were waited for; matrix products, arithmetic and copies ran while one was open for 1% of the time, Pallas kernels for 8%

profile of v4, /device:TPU:8, one launch (start us, length us, event | category | flops | bytes accessed | tf_op | source)
XLA Modules:
  0.0 137.5 jit_solution(7033973269985494665)
XLA Ops:
  0.0 3.0 %collective-permute-start = (bf16[4,6144]{1,0:T(4,128)(2,1)}, bf16[4,6144]{1,0:T(4,128)(2,1)}, u32[]{:S(2)}, u32[]{:S(2)}) collective-permute-start(bf16[4,6144]{1,0:T(4,128)(2,1)} %tokens.3), channel_id=1, source_target_pairs={{0,2},{2,0},{1,3},{3,1},{4,6},{6,4},{5,7},{7,5},{8,10},{10,8},{9,1... | collective-permute-start | bytes 147464 | tf_op jit(solution)/shard_map/ppermute | solution.py:30
  3.0 2.9 %collective-permute-done.received = bf16[4,6144]{1,0:T(4,128)(2,1)} collective-permute-done((bf16[4,6144]{1,0:T(4,128)(2,1)}, bf16[4,6144]{1,0:T(4,128)(2,1)}, u32[]{:S(2)}, u32[]{:S(2)}) %collective-permute-start) | collective-permute-done | bytes 49184 | tf_op jit(solution)/shard_map/ppermute | solution.py:30
  5.9 2.1 %normed_pieces.1 = bf16[32,8,1536]{2,1,0:T(8,128)(2,1)} custom-call(bf16[4,6144]{1,0:T(4,128)(2,1)} %tokens.3, bf16[4,6144]{1,0:T(4,128)(2,1)} %collective-permute-done.received, f32[1,6144]{1,0:T(1,128)} %bitcast.5), custom_call_target="tpu_custom_call" | custom-call | flops 491520 | bytes 2097152 | tf_op jit(solution)/shard_map/normed_pieces/pallas_call | solution.py:80
  8.0 0.0 copy-start.4
  8.0 0.0 copy-start.5
  8.0 0.0 copy-start.6
  8.0 0.0 copy-start.3
  8.1 11.8 %all-to-all-start = ((bf16[32,8,1536]{2,1,0:T(8,128)(2,1)}), bf16[32,8,1536]{2,1,0:T(8,128)(2,1)S(1)}, u32[]{:S(2)}, u32[]{:S(2)}) async-start(bf16[32,8,1536]{2,1,0:T(8,128)(2,1)} %normed_pieces.1), calls=%async_computation | async-start | bytes 1572864 | tf_op jit(solution)/shard_map/all_to_all | solution.py:34
  19.9 1.6 %collective-permute-start.3 = (bf16[768,768]{1,0:T(8,128)(2,1)}, bf16[768,768]{1,0:T(8,128)(2,1)}, u32[]{:S(2)}, u32[]{:S(2)}) collective-permute-start(bf16[768,768]{1,0:T(8,128)(2,1)} %w_own.3), channel_id=1, source_target_pairs={{0,128},{128,0},{1,129},{129,1},{2,130},{130,2},{3,131},{131,3},{4... | collective-permute-start | bytes 3538952 | tf_op jit(solution)/shard_map/ppermute | solution.py:30
  21.5 17.8 %all-to-all-done = bf16[32,8,1536]{2,1,0:T(8,128)(2,1)S(1)} async-done(((bf16[32,8,1536]{2,1,0:T(8,128)(2,1)}), bf16[32,8,1536]{2,1,0:T(8,128)(2,1)S(1)}, u32[]{:S(2)}, u32[]{:S(2)}) %all-to-all-start) | async-done | bytes 786464 | tf_op jit(solution)/shard_map/all_to_all | solution.py:34
  39.3 0.0 collective-permute-start.1
  39.3 0.0 copy-done.4
  39.3 0.0 copy-done.5
  39.4 0.0 copy-done.6
  39.5 1.6 %collective-permute-start.2 = (bf16[768,384]{1,0:T(8,128)(2,1)S(1)}, bf16[768,384]{1,0:T(8,128)(2,1)S(1)}, u32[]{:S(2)}, u32[]{:S(2)}) collective-permute-start(bf16[768,384]{1,0:T(8,128)(2,1)S(1)} %constant_dynamic-update-slice_fusion.w_own), channel_id=1, source_target_pairs={{0,128},{128,0},{1,129},{129,1},{2,130},{130,2},{3,131},{131,3},{4... | collective-permute-start | bytes 1769480 | tf_op jit(solution)/shard_map/ppermute | solution.py:30
  41.0 0.9 constant_dynamic-update-slice_fusion.4
  42.0 0.0 copy-done.3
  42.0 0.1 constant_dynamic-update-slice_fusion.3.w_own
  42.1 0.6 collective-permute-start.4
  42.7 6.5 %collective-permute-done.3.w_other = bf16[768,768]{1,0:T(8,128)(2,1)} collective-permute-done((bf16[768,768]{1,0:T(8,128)(2,1)}, bf16[768,768]{1,0:T(8,128)(2,1)}, u32[]{:S(2)}, u32[]{:S(2)}) %collective-permute-start.3) | collective-permute-done | bytes 1179680 | tf_op jit(solution)/shard_map/ppermute | solution.py:30
  49.2 2.7 %inner_part.2.inner_mine = bf16[4,64,768]{2,1,0:T(8,128)(2,1)S(1)} custom-call(bf16[4,64,1536]{2,1,0:T(8,128)(2,1)S(1)} %bitcast.3, bf16[768,768]{1,0:T(8,128)(2,1)} %w_own.3, bf16[768,768]{1,0:T(8,128)(2,1)} %collective-permute-done.3.w_other), custom_call_target="tpu_custom_call" | custom-call | flops 603979776 | bytes 4194304 | tf_op jit(solution)/shard_map/inner_part/pallas_call | solution.py:123
  51.8 0.0 collective-permute-done.1.tokens.theirs
  51.9 2.7 %inner_part.3.inner_theirs = bf16[4,64,768]{2,1,0:T(8,128)(2,1)S(1)} custom-call(bf16[4,64,1536]{2,1,0:T(8,128)(2,1)S(1)} %collective-permute-done.1.tokens.theirs, bf16[768,768]{1,0:T(8,128)(2,1)} %w_own.3, bf16[768,768]{1,0:T(8,128)(2,1)} %collective-permute-done.3.w_other), custom_call_target="tpu_custom_call" | custom-call | flops 603979776 | bytes 4194304 | tf_op jit(solution)/shard_map/inner_part/pallas_call | solution.py:123
  54.5 7.1 %collective-permute-done.2.w_other = bf16[768,384]{1,0:T(8,128)(2,1)S(1)} collective-permute-done((bf16[768,384]{1,0:T(8,128)(2,1)S(1)}, bf16[768,384]{1,0:T(8,128)(2,1)S(1)}, u32[]{:S(2)}, u32[]{:S(2)}) %collective-permute-start.2) | collective-permute-done | bytes 589856 | tf_op jit(solution)/shard_map/ppermute | solution.py:30
  61.7 1.6 %heads_part.1 = bf16[4,128,1152]{2,1,0:T(8,128)(2,1)S(1)} custom-call(bf16[4,64,1536]{2,1,0:T(8,128)(2,1)S(1)} %bitcast.4, bf16[4,64,1536]{2,1,0:T(8,128)(2,1)S(1)} %collective-permute-done.1.tokens.theirs, bf16[768,384]{1,0:T(8,128)(2,1)S(1)} %constant_dynamic-update-slice_fusion.w_own, bf16[768,384]{1,0:T(8,128)(2,1)S(1)} %collective-permute-done.2.w_other, ...), custom_call_target="tpu_custom_call" | custom-call | flops 603979776 | bytes 4194304 | tf_op jit(solution)/shard_map/heads_part/pallas_call | solution.py:172
  63.3 0.0 copy-start
  63.3 1.0 copy-done
  64.3 0.0 copy-start.2
  64.3 4.9 %all-to-all-start.1 = ((bf16[4,128,1152]{2,1,0:T(8,128)(2,1)}), bf16[4,128,1152]{2,1,0:T(8,128)(2,1)}, u32[]{:S(2)}, u32[]{:S(2)}) async-start(bf16[4,128,1152]{2,1,0:T(8,128)(2,1)} %copy-done), calls=%async_computation.1 | async-start | bytes 2359296 | tf_op jit(solution)/shard_map/all_to_all | solution.py:34
  69.9 10.9 %all-to-all-done.1.arrived = bf16[4,128,1152]{2,1,0:T(8,128)(2,1)} async-done(((bf16[4,128,1152]{2,1,0:T(8,128)(2,1)}), bf16[4,128,1152]{2,1,0:T(8,128)(2,1)}, u32[]{:S(2)}, u32[]{:S(2)}) %all-to-all-start.1) | async-done | bytes 1179680 | tf_op jit(solution)/shard_map/all_to_all | solution.py:34
  80.8 0.0 copy-done.2
  80.8 2.1 %middle.1 = bf16[1,128,896]{2,1,0:T(8,128)(2,1)S(1)} custom-call(bf16[4,128,1152]{2,1,0:T(8,128)(2,1)} %all-to-all-done.1.arrived, f32[768]{0:T(1024)S(1)} %copy-done.2, f32[1]{0:T(128)S(6)} %div.3.scale), custom_call_target="tpu_custom_call" | custom-call | flops 5898240 | bytes 2097152 | tf_op jit(solution)/shard_map/middle/pallas_call | solution.py:223
  82.9 13.2 %all_gather.3.features = bf16[4,128,896]{2,1,0:T(8,128)(2,1)S(1)} all-gather(bf16[1,128,896]{2,1,0:T(8,128)(2,1)S(1)} %middle.1), channel_id=1, replica_groups=mesh['xl'=2,'y'=4,'z'=8,'xh'=2,'c'=2] {'y'}, dimensions={0}, use_global_device_ids=true | all-gather | bytes 1146880 | tf_op jit(solution)/shard_map/all_gather | solution.py:325
  96.1 0.0 collective-permute-done.4.w_other
  96.1 1.8 %output_sent.1 = bf16[4,64,1536]{2,1,0:T(8,128)(2,1)S(1)} custom-call(bf16[4,128,896]{2,1,0:T(8,128)(2,1)S(1)} %all_gather.3.features, bf16[896,768]{1,0:T(8,128)(2,1)S(1)} %constant_dynamic-update-slice_fusion.3.w_own, bf16[896,768]{1,0:T(8,128)(2,1)S(1)} %collective-permute-done.4.w_other), custom_call_target="tpu_custom_call" | custom-call | flops 704643072 | bytes 4194304 | tf_op jit(solution)/shard_map/output_sent/pallas_call | solution.py:260
  97.9 0.1 collective-permute-start.5
  98.0 1.8 %output_kept.1 = f32[4,64,1536]{2,1,0:T(8,128)S(1)} custom-call(bf16[4,128,896]{2,1,0:T(8,128)(2,1)S(1)} %all_gather.3.features, bf16[896,768]{1,0:T(8,128)(2,1)S(1)} %constant_dynamic-update-slice_fusion.3.w_own, bf16[896,768]{1,0:T(8,128)(2,1)S(1)} %collective-permute-done.4.w_other), custom_call_target="tpu_custom_call" | custom-call | flops 704643072 | bytes 4194304 | tf_op jit(solution)/shard_map/output_kept/pallas_call | solution.py:260
  99.9 0.4 collective-permute-done.5
  100.3 0.2 add_convert_fusion
  100.5 0.0 copy-start.1
  100.5 0.2 reshape.11
  100.7 35.9 %all_to_all.15.arrived = bf16[64,4,1536]{2,1,0:T(4,128)(2,1)S(1)} all-to-all(bf16[64,4,1536]{2,1,0:T(4,128)(2,1)S(1)} %reshape.11), channel_id=1, replica_groups=mesh['xl'=2,'y'=4,'z'=8,'xh'=2,'c'=2] {'y','z','xh'}, dimensions={0} | all-to-all | bytes 1572864 | tf_op jit(solution)/shard_map/all_to_all | solution.py:34
  136.6 0.0 copy-done.1
  136.6 1.0 finish.1
  (3 shorter events, 0.1 us)
Async XLA Ops:
  0.0 5.9 %collective-permute-start = (bf16[4,6144]{1,0:T(4,128)(2,1)}, bf16[4,6144]{1,0:T(4,128)(2,1)}, u32[]{:S(2)}, u32[]{:S(2)}) collective-permute-start(bf16[4,6144]{1,0:T(4,128)(2,1)} %tokens.3), channel_id=1, source_target_pairs={{0,2},{2,0},{1,3},{3,1},{4,6},{6,4},{5,7},{7,5},{8,10},{10,8},{9,1... | collective-permute-start | bytes 147464 | tf_op jit(solution)/shard_map/ppermute | solution.py:30
  8.0 31.3 %copy-start.4 = (bf16[768,128]{1,0:T(8,128)(2,1)S(1)}, bf16[768,128]{1,0:T(8,128)(2,1)}, u32[]{:S(2)}) copy-start(bf16[768,128]{1,0:T(8,128)(2,1)} %param.12) | copy-start | bytes 589828
  8.0 31.3 %copy-start.5 = (bf16[768,128]{1,0:T(8,128)(2,1)S(1)}, bf16[768,128]{1,0:T(8,128)(2,1)}, u32[]{:S(2)}) copy-start(bf16[768,128]{1,0:T(8,128)(2,1)} %param.13) | copy-start | bytes 589828
  8.0 31.4 %copy-start.6 = (bf16[768,128]{1,0:T(8,128)(2,1)S(1)}, bf16[768,128]{1,0:T(8,128)(2,1)}, u32[]{:S(2)}) copy-start(bf16[768,128]{1,0:T(8,128)(2,1)} %param.14) | copy-start | bytes 589828
  8.0 33.9 %copy-start.3 = (bf16[768,768]{1,0:T(8,128)(2,1)S(1)}, bf16[768,768]{1,0:T(8,128)(2,1)}, u32[]{:S(2)}) copy-start(bf16[768,768]{1,0:T(8,128)(2,1)} %param.18) | copy-start | bytes 3538948
  8.1 31.2 %all-to-all-start = ((bf16[32,8,1536]{2,1,0:T(8,128)(2,1)}), bf16[32,8,1536]{2,1,0:T(8,128)(2,1)S(1)}, u32[]{:S(2)}, u32[]{:S(2)}) async-start(bf16[32,8,1536]{2,1,0:T(8,128)(2,1)} %normed_pieces.1), calls=%async_computation | async-start | bytes 1572864 | tf_op jit(solution)/shard_map/all_to_all | solution.py:34
  19.9 29.2 %collective-permute-start.3 = (bf16[768,768]{1,0:T(8,128)(2,1)}, bf16[768,768]{1,0:T(8,128)(2,1)}, u32[]{:S(2)}, u32[]{:S(2)}) collective-permute-start(bf16[768,768]{1,0:T(8,128)(2,1)} %w_own.3), channel_id=1, source_target_pairs={{0,128},{128,0},{1,129},{129,1},{2,130},{130,2},{3,131},{131,3},{4... | collective-permute-start | bytes 3538952 | tf_op jit(solution)/shard_map/ppermute | solution.py:30
  39.3 12.6 %collective-permute-start.1 = (bf16[4,64,1536]{2,1,0:T(8,128)(2,1)S(1)}, bf16[4,64,1536]{2,1,0:T(8,128)(2,1)S(1)}, u32[]{:S(2)}, u32[]{:S(2)}) collective-permute-start(bf16[4,64,1536]{2,1,0:T(8,128)(2,1)S(1)} %bitcast.2), channel_id=1, source_target_pairs={{0,1},{1,0},{2,3},{3,2},{4,5},{5,4},{6,7},{7,6},{8,9},{9,8},{10,11... | collective-permute-start | bytes 2359304 | tf_op jit(solution)/shard_map/ppermute | solution.py:30
  39.5 22.2 %collective-permute-start.2 = (bf16[768,384]{1,0:T(8,128)(2,1)S(1)}, bf16[768,384]{1,0:T(8,128)(2,1)S(1)}, u32[]{:S(2)}, u32[]{:S(2)}) collective-permute-start(bf16[768,384]{1,0:T(8,128)(2,1)S(1)} %constant_dynamic-update-slice_fusion.w_own), channel_id=1, source_target_pairs={{0,128},{128,0},{1,129},{129,1},{2,130},{130,2},{3,131},{131,3},{4... | collective-permute-start | bytes 1769480 | tf_op jit(solution)/shard_map/ppermute | solution.py:30
  42.1 54.0 %collective-permute-start.4 = (bf16[896,768]{1,0:T(8,128)(2,1)S(1)}, bf16[896,768]{1,0:T(8,128)(2,1)S(1)}, u32[]{:S(2)}, u32[]{:S(2)}) collective-permute-start(bf16[896,768]{1,0:T(8,128)(2,1)S(1)} %constant_dynamic-update-slice_fusion.3.w_own), channel_id=1, source_target_pairs={{0,128},{128,0},{1,129},{129,1},{2,130},{130,2},{3,131},{131,3},{4... | collective-permute-start | bytes 4128776 | tf_op jit(solution)/shard_map/ppermute | solution.py:30
  63.3 1.0 copy-start
  64.3 16.4 %copy-start.2 = (f32[768]{0:T(1024)S(1)}, f32[768]{0:T(1024)}, u32[]{:S(2)}) copy-start(f32[768]{0:T(1024)} %bias.1) | copy-start | bytes 9220
  64.3 16.4 %all-to-all-start.1 = ((bf16[4,128,1152]{2,1,0:T(8,128)(2,1)}), bf16[4,128,1152]{2,1,0:T(8,128)(2,1)}, u32[]{:S(2)}, u32[]{:S(2)}) async-start(bf16[4,128,1152]{2,1,0:T(8,128)(2,1)} %copy-done), calls=%async_computation.1 | async-start | bytes 2359296 | tf_op jit(solution)/shard_map/all_to_all | solution.py:34
  97.9 2.4 %collective-permute-start.5 = (bf16[4,64,1536]{2,1,0:T(8,128)(2,1)S(1)}, bf16[4,64,1536]{2,1,0:T(8,128)(2,1)S(1)}, u32[]{:S(2)}, u32[]{:S(2)}) collective-permute-start(bf16[4,64,1536]{2,1,0:T(8,128)(2,1)S(1)} %output_sent.1), channel_id=1, source_target_pairs={{0,1},{1,0},{2,3},{3,2},{4,5},{5,4},{6,7},{7,6},{8,9},{9,8},{10,11... | collective-permute-start | bytes 2359304 | tf_op jit(solution)/shard_map/ppermute | solution.py:30
  100.5 36.1 %copy-start.1 = (bf16[4,6144]{1,0:T(4,128)(2,1)S(1)}, bf16[4,6144]{1,0:T(4,128)(2,1)}, u32[]{:S(2)}) copy-start(bf16[4,6144]{1,0:T(4,128)(2,1)} %tokens.3) | copy-start | bytes 147460

commit v5 on v4

--- a/solution.py
+++ b/solution.py
@@ -46,24 +46,45 @@
     return pl.CostEstimate(flops=flops, bytes_accessed=moved, transcendentals=0)
 
 
-def spread_kernel(n_y, n_z, tokens, received, norm_gain, out, own, beside, gain, sems):
-    _, width = own.shape
-    cols = width // (2 * n_y)
+def norm_kernel(tokens, norm_gain, normed, gain, own, sems):
     copies = [
         pltpu.make_async_copy(tokens, own, sems.at[0]),
-        pltpu.make_async_copy(received, beside, sems.at[1]),
-        pltpu.make_async_copy(norm_gain, gain, sems.at[2]),
+        pltpu.make_async_copy(norm_gain, gain, sems.at[1]),
     ]
     for copy in copies:
         copy.start()
-    for copy in copies:
-        copy.wait()
-    mine, theirs = own[...].astype(F32), beside[...].astype(F32)
+    copies[0].wait()
+    values = normalize(own[...].astype(F32))
+    copies[1].wait()
+    normed[...] = values * gain[...]
+
+
+def norm_own(tokens, gain):
+    count, width = tokens.shape
+    return pl.pallas_call(
+        norm_kernel,
+        out_shape=(
+            jax.ShapeDtypeStruct((count, width), F32),
+            jax.ShapeDtypeStruct((1, width), F32),
+        ),
+        in_specs=[ANY] * 2,
+        out_specs=(VMEM, VMEM),
+        scratch_shapes=[pltpu.VMEM((count, width), BF), pltpu.SemaphoreType.DMA((2,))],
+        compiler_params=params(8),
+        cost_estimate=cost(100 * count * width, 1024 * 1024),
+        name="norm_own",
+    )(tokens, gain.reshape(1, width))
+
+
+def spread_kernel(n_y, n_z, normed_own, gain, beside, out):
+    _, width = beside.shape
+    cols = width // (2 * n_y)
+    mine = normed_own[...]
+    theirs = normalize(beside[...].astype(F32)) * gain[...]
     first = lax.axis_index("xh") == 0
-    rows = jnp.concatenate(
+    normed = jnp.concatenate(
         (jnp.where(first, mine, theirs), jnp.where(first, theirs, mine)), axis=0
     )
-    normed = normalize(rows) * gain[...]
     lower = lax.axis_index("xl") == 0
     for y in range(n_y):
         a = normed[:, y * cols : (y + 1) * cols]
@@ -75,23 +96,17 @@
             out[y * n_z + z, :, cols:] = right
 
 
-def spread(tokens, beside, gain, n_y, n_z):
-    count, width = tokens.shape
+def spread(normed_own, gain, beside, n_y, n_z):
+    count, width = beside.shape
     return pl.pallas_call(
         functools.partial(spread_kernel, n_y, n_z),
         out_shape=jax.ShapeDtypeStruct((n_y * n_z, 2 * count, width // n_y), BF),
-        in_specs=[ANY] * 3,
-        out_specs=VMEM,
-        scratch_shapes=[
-            pltpu.VMEM((count, width), BF),
-            pltpu.VMEM((count, width), BF),
-            pltpu.VMEM((1, width), F32),
-            pltpu.SemaphoreType.DMA((3,)),
-        ],
-        compiler_params=pltpu.CompilerParams(vmem_limit_bytes=67_000_000),
+        in_specs=[VMEM] * 3,
+        out_specs=VMEM,
+        compiler_params=params(8),
         cost_estimate=cost(20 * count * width, 2 * 1024 * 1024),
         name="normed_pieces",
-    )(tokens, beside, gain.reshape(1, width))
+    )(normed_own, gain, beside)
 
 
 def product(rows, w, w_p, at):
@@ -100,21 +115,28 @@
 
 
 def inner_kernel(tokens, w_own, w_other, out, rows, kept, kept_p, sems):
-    copies = [
-        pltpu.make_async_copy(tokens, rows, sems.at[0]),
-        pltpu.make_async_copy(w_own, kept, sems.at[1]),
-        pltpu.make_async_copy(w_other, kept_p, sems.at[2]),
-    ]
-    for copy in copies:
+    images, half, width = rows.shape
+    chunk = 384
+    first = pltpu.make_async_copy(tokens, rows, sems.at[0])
+    copies = []
+    for n in range(kept.shape[1] // chunk):
+        at = pl.ds(n * chunk, chunk)
+        for m, (source, to) in enumerate(((w_own, kept), (w_other, kept_p))):
+            copies.append(
+                pltpu.make_async_copy(source.at[:, at], to.at[:, at], sems.at[1 + 2 * n + m])
+            )
+    copies[0].start()
+    first.start()
+    for copy in copies[1:]:
         copy.start()
-    for copy in copies:
-        copy.wait()
-    images, half, width = rows.shape
+    first.wait()
     left = rows[...].reshape(images * half, width)
-    for n in range(kept.shape[1] // 384):
-        at = slice(n * 384, (n + 1) * 384)
+    for n in range(kept.shape[1] // chunk):
+        copies[2 * n].wait()
+        copies[2 * n + 1].wait()
+        at = slice(n * chunk, (n + 1) * chunk)
         value = product(left, kept, kept_p, at)
-        out[:, :, at] = value.astype(BF).reshape(images, half, 384)
+        out[:, :, at] = value.astype(BF).reshape(images, half, chunk)
 
 
 def inner_part(tokens, w_own, w_other):
@@ -129,7 +151,7 @@
             pltpu.VMEM(tokens.shape, BF),
             pltpu.VMEM(w_own.shape, BF),
             pltpu.VMEM(w_other.shape, BF),
-            pltpu.SemaphoreType.DMA((3,)),
+            pltpu.SemaphoreType.DMA((5,)),
         ],
         compiler_params=params(12),
         cost_estimate=cost(2 * images * half * width * columns, 4 * 1024 * 1024),
@@ -152,16 +174,19 @@
     ]
     for copy in copies:
         copy.start()
-    for copy in copies[:3]:
-        copy.wait()
-    for part, source in enumerate((rows, rows_p)):
-        if part:
-            copies[3].wait()
-        left = source[...].reshape(images * half, width)
-        value = product(left, kept, kept_p, slice(0, wide))
-        out[:, part * half : (part + 1) * half, :wide] = value.astype(BF).reshape(
-            images, half, wide
-        )
+    cols = width // 2
+    copies[0].wait()
+    copies[1].wait()
+    left = rows[...].reshape(images * half, width)
+    own = dot(left[:, :cols], kept[...])
+    copies[2].wait()
+    out[:, :half, :wide] = (
+        (own + dot(left[:, cols:], kept_p[...])).astype(BF).reshape(images, half, wide)
+    )
+    copies[3].wait()
+    left = rows_p[...].reshape(images * half, width)
+    value = dot(left[:, :cols], kept[...]) + dot(left[:, cols:], kept_p[...])
+    out[:, half:, :wide] = value.astype(BF).reshape(images, half, wide)
     for copy in copies[4:]:
         copy.wait()
 
@@ -312,7 +337,8 @@
     w_qkv_p = partner(w_qkv, "xl")
     w_out = jnp.concatenate((w_attn_out, w_outer), axis=0)
     w_out_p = partner(w_out, "xl")
-    pieces = spread(tokens, beside, norm_gain, n_y, n_z)
+    normed, gain = norm_own(tokens, norm_gain)
+    pieces = spread(normed, gain, beside, n_y, n_z)
     mine = exchange(pieces, ("y", "z"))
     mine = mine.reshape(n_y, -1, mine.shape[-1])
     theirs = partner(mine, "c")

time: 138 us -> 137 us (level)
  waiting for transfers between devices: 45.6 us -> 44 us
  local copies, waits for them, and re-layouts: 2.38 us -> 3.92 us
    ppermute x6, waiting for transfers between devices: 16.9 us -> 15.2 us  [partner(): return lax.ppermute(array, axis, [(0, 1), (1, 0)])]
    unnamed x17 -> x21, local copies, waits for them, and re-layouts: 2.07 us -> 3.61 us
where the time goes in v5:
time: 137 us
  blocking collectives  49 us (36%)
  waiting for transfers between devices  44 us (32%)
  starting transfers between devices  23.7 us (17%)
  Pallas kernels  15 us (11%)
  local copies, waits for them, and re-layouts  3.92 us (3%)
    all_to_all x1, blocking collectives, exchange(): return lax.all_to_all(pieces, axes, split_axis=0, concat_axis=0, tiled=True)  35.7 us
    all_to_all x2, waiting for transfers between devices, exchange(): return lax.all_to_all(pieces, axes, split_axis=0, concat_axis=0, tiled=True)  28.8 us
    all_to_all x2, starting transfers between devices, exchange(): return lax.all_to_all(pieces, axes, split_axis=0, concat_axis=0, tiled=True)  16.8 us
    ppermute x6, waiting for transfers between devices, partner(): return lax.ppermute(array, axis, [(0, 1), (1, 0)])  15.2 us
    all_gather x1, blocking collectives, block(): features = lax.all_gather(features, 'y', axis=0, tiled=False)  13.3 us
    ppermute x6, starting transfers between devices, partner(): return lax.ppermute(array, axis, [(0, 1), (1, 0)])  6.9 us
    pallas_call x2, Pallas kernels, inner_part(): pl.pallas_call(inner_kernel, out_shape=jax.ShapeDtypeStruct((images, half...  4.93 us
    pallas_call x2, Pallas kernels, output(): pl.pallas_call(functools.partial(output_kernel, part), out_shape=jax.Shap...  3.67 us
  transfers between devices with their start and end apart: 8, of which 6 were waited for; matrix products, arithmetic and copies ran while one was open for 1% of the time, Pallas kernels for 8%

profile of v5, /device:TPU:8, one launch (start us, length us, event | category | flops | bytes accessed | tf_op | source)
XLA Modules:
  0.0 136.6 jit_solution(2175963990996882954)
XLA Ops:
  0.0 3.0 %collective-permute-start = (bf16[4,6144]{1,0:T(4,128)(2,1)}, bf16[4,6144]{1,0:T(4,128)(2,1)S(1)}, u32[]{:S(2)}, u32[]{:S(2)}) collective-permute-start(bf16[4,6144]{1,0:T(4,128)(2,1)} %tokens.3), channel_id=1, source_target_pairs={{0,2},{2,0},{1,3},{3,1},{4,6},{6,4},{5,7},{7,5},{8,10},{10,8},{9,1... | collective-permute-start | bytes 147464 | tf_op jit(solution)/shard_map/ppermute | solution.py:30
  3.0 0.0 copy-start.1
  3.0 0.8 copy-done.1
  3.9 0.0 copy-start.3
  3.9 0.7 copy-done.3
  4.6 0.4 norm_own.1
  5.0 0.8 collective-permute-done.beside
  5.8 0.0 copy-start.7
  5.8 1.2 normed_pieces.1
  7.0 0.0 copy-start.8
  7.0 0.0 copy-start.5
  7.0 11.8 %all-to-all-start = ((bf16[32,8,1536]{2,1,0:T(8,128)(2,1)}), bf16[32,8,1536]{2,1,0:T(8,128)(2,1)S(1)}, u32[]{:S(2)}, u32[]{:S(2)}) async-start(bf16[32,8,1536]{2,1,0:T(8,128)(2,1)} %normed_pieces.1), calls=%async_computation | async-start | bytes 1572864 | tf_op jit(solution)/shard_map/all_to_all | solution.py:34
  18.9 1.6 %collective-permute-start.3 = (bf16[768,768]{1,0:T(8,128)(2,1)}, bf16[768,768]{1,0:T(8,128)(2,1)}, u32[]{:S(2)}, u32[]{:S(2)}) collective-permute-start(bf16[768,768]{1,0:T(8,128)(2,1)} %w_own.3), channel_id=1, source_target_pairs={{0,128},{128,0},{1,129},{129,1},{2,130},{130,2},{3,131},{131,3},{4... | collective-permute-start | bytes 3538952 | tf_op jit(solution)/shard_map/ppermute | solution.py:30
  20.5 17.9 %all-to-all-done = bf16[32,8,1536]{2,1,0:T(8,128)(2,1)S(1)} async-done(((bf16[32,8,1536]{2,1,0:T(8,128)(2,1)}), bf16[32,8,1536]{2,1,0:T(8,128)(2,1)S(1)}, u32[]{:S(2)}, u32[]{:S(2)}) %all-to-all-start) | async-done | bytes 786464 | tf_op jit(solution)/shard_map/all_to_all | solution.py:34
  38.3 0.0 collective-permute-start.1
  38.3 0.0 copy-done.6
  38.4 0.0 copy-done.7
  38.5 0.0 copy-done.8
  38.5 1.5 %collective-permute-start.2 = (bf16[768,384]{1,0:T(8,128)(2,1)S(1)}, bf16[768,384]{1,0:T(8,128)(2,1)S(1)}, u32[]{:S(2)}, u32[]{:S(2)}) collective-permute-start(bf16[768,384]{1,0:T(8,128)(2,1)S(1)} %constant_dynamic-update-slice_fusion.w_own), channel_id=1, source_target_pairs={{0,128},{128,0},{1,129},{129,1},{2,130},{130,2},{3,131},{131,3},{4... | collective-permute-start | bytes 1769480 | tf_op jit(solution)/shard_map/ppermute | solution.py:30
  40.0 0.9 constant_dynamic-update-slice_fusion.4
  41.0 0.0 copy-done.5
  41.0 0.1 constant_dynamic-update-slice_fusion.3.w_own
  41.1 0.7 collective-permute-start.4
  41.8 6.4 %collective-permute-done.3.w_other = bf16[768,768]{1,0:T(8,128)(2,1)} collective-permute-done((bf16[768,768]{1,0:T(8,128)(2,1)}, bf16[768,768]{1,0:T(8,128)(2,1)}, u32[]{:S(2)}, u32[]{:S(2)}) %collective-permute-start.3) | collective-permute-done | bytes 1179680 | tf_op jit(solution)/shard_map/ppermute | solution.py:30
  48.1 2.5 %inner_part.2.inner_mine = bf16[4,64,768]{2,1,0:T(8,128)(2,1)S(1)} custom-call(bf16[4,64,1536]{2,1,0:T(8,128)(2,1)S(1)} %bitcast.3, bf16[768,768]{1,0:T(8,128)(2,1)} %w_own.3, bf16[768,768]{1,0:T(8,128)(2,1)} %collective-permute-done.3.w_other), custom_call_target="tpu_custom_call" | custom-call | flops 603979776 | bytes 4194304 | tf_op jit(solution)/shard_map/inner_part/pallas_call | solution.py:145
  50.6 0.0 collective-permute-done.1.tokens.theirs
  50.6 2.5 %inner_part.3.inner_theirs = bf16[4,64,768]{2,1,0:T(8,128)(2,1)S(1)} custom-call(bf16[4,64,1536]{2,1,0:T(8,128)(2,1)S(1)} %collective-permute-done.1.tokens.theirs, bf16[768,768]{1,0:T(8,128)(2,1)} %w_own.3, bf16[768,768]{1,0:T(8,128)(2,1)} %collective-permute-done.3.w_other), custom_call_target="tpu_custom_call" | custom-call | flops 603979776 | bytes 4194304 | tf_op jit(solution)/shard_map/inner_part/pallas_call | solution.py:145
  53.1 7.6 %collective-permute-done.2.w_other = bf16[768,384]{1,0:T(8,128)(2,1)S(1)} collective-permute-done((bf16[768,384]{1,0:T(8,128)(2,1)S(1)}, bf16[768,384]{1,0:T(8,128)(2,1)S(1)}, u32[]{:S(2)}, u32[]{:S(2)}) %collective-permute-start.2) | collective-permute-done | bytes 589856 | tf_op jit(solution)/shard_map/ppermute | solution.py:30
  60.7 1.7 %heads_part.1 = bf16[4,128,1152]{2,1,0:T(8,128)(2,1)S(1)} custom-call(bf16[4,64,1536]{2,1,0:T(8,128)(2,1)S(1)} %bitcast.4, bf16[4,64,1536]{2,1,0:T(8,128)(2,1)S(1)} %collective-permute-done.1.tokens.theirs, bf16[768,384]{1,0:T(8,128)(2,1)S(1)} %constant_dynamic-update-slice_fusion.w_own, bf16[768,384]{1,0:T(8,128)(2,1)S(1)} %collective-permute-done.2.w_other, ...), custom_call_target="tpu_custom_call" | custom-call | flops 603979776 | bytes 4194304 | tf_op jit(solution)/shard_map/heads_part/pallas_call | solution.py:197
  62.4 0.0 copy-start
  62.4 1.0 copy-done
  63.4 0.0 copy-start.4
  63.4 4.9 %all-to-all-start.1 = ((bf16[4,128,1152]{2,1,0:T(8,128)(2,1)}), bf16[4,128,1152]{2,1,0:T(8,128)(2,1)}, u32[]{:S(2)}, u32[]{:S(2)}) async-start(bf16[4,128,1152]{2,1,0:T(8,128)(2,1)} %copy-done), calls=%async_computation.1 | async-start | bytes 2359296 | tf_op jit(solution)/shard_map/all_to_all | solution.py:34
  69.0 11.0 %all-to-all-done.1.arrived = bf16[4,128,1152]{2,1,0:T(8,128)(2,1)} async-done(((bf16[4,128,1152]{2,1,0:T(8,128)(2,1)}), bf16[4,128,1152]{2,1,0:T(8,128)(2,1)}, u32[]{:S(2)}, u32[]{:S(2)}) %all-to-all-start.1) | async-done | bytes 1179680 | tf_op jit(solution)/shard_map/all_to_all | solution.py:34
  79.9 0.0 copy-done.4
  79.9 2.1 %middle.1 = bf16[1,128,896]{2,1,0:T(8,128)(2,1)S(1)} custom-call(bf16[4,128,1152]{2,1,0:T(8,128)(2,1)} %all-to-all-done.1.arrived, f32[768]{0:T(1024)S(1)} %copy-done.4, f32[1]{0:T(128)S(6)} %div.3.scale), custom_call_target="tpu_custom_call" | custom-call | flops 5898240 | bytes 2097152 | tf_op jit(solution)/shard_map/middle/pallas_call | solution.py:248
  82.1 13.3 %all_gather.3.features = bf16[4,128,896]{2,1,0:T(8,128)(2,1)S(1)} all-gather(bf16[1,128,896]{2,1,0:T(8,128)(2,1)S(1)} %middle.1), channel_id=1, replica_groups=mesh['xl'=2,'y'=4,'z'=8,'xh'=2,'c'=2] {'y'}, dimensions={0}, use_global_device_ids=true | all-gather | bytes 1146880 | tf_op jit(solution)/shard_map/all_gather | solution.py:351
  95.3 0.0 collective-permute-done.4.w_other
  95.3 1.8 %output_sent.1 = bf16[4,64,1536]{2,1,0:T(8,128)(2,1)S(1)} custom-call(bf16[4,128,896]{2,1,0:T(8,128)(2,1)S(1)} %all_gather.3.features, bf16[896,768]{1,0:T(8,128)(2,1)S(1)} %constant_dynamic-update-slice_fusion.3.w_own, bf16[896,768]{1,0:T(8,128)(2,1)S(1)} %collective-permute-done.4.w_other), custom_call_target="tpu_custom_call" | custom-call | flops 704643072 | bytes 4194304 | tf_op jit(solution)/shard_map/output_sent/pallas_call | solution.py:285
  97.2 0.1 collective-permute-start.5
  97.3 1.8 %output_kept.1 = f32[4,64,1536]{2,1,0:T(8,128)S(1)} custom-call(bf16[4,128,896]{2,1,0:T(8,128)(2,1)S(1)} %all_gather.3.features, bf16[896,768]{1,0:T(8,128)(2,1)S(1)} %constant_dynamic-update-slice_fusion.3.w_own, bf16[896,768]{1,0:T(8,128)(2,1)S(1)} %collective-permute-done.4.w_other), custom_call_target="tpu_custom_call" | custom-call | flops 704643072 | bytes 4194304 | tf_op jit(solution)/shard_map/output_kept/pallas_call | solution.py:285
  99.1 0.4 collective-permute-done.5
  99.5 0.2 add_convert_fusion
  99.7 0.0 copy-start.2
  99.7 0.2 reshape.11
  99.9 35.7 %all_to_all.15.arrived = bf16[64,4,1536]{2,1,0:T(4,128)(2,1)S(1)} all-to-all(bf16[64,4,1536]{2,1,0:T(4,128)(2,1)S(1)} %reshape.11), channel_id=1, replica_groups=mesh['xl'=2,'y'=4,'z'=8,'xh'=2,'c'=2] {'y','z','xh'}, dimensions={0} | all-to-all | bytes 1572864 | tf_op jit(solution)/shard_map/all_to_all | solution.py:34
  135.6 0.0 copy-done.2
  135.6 1.0 finish.1
  (4 shorter events, 0.1 us)
Async XLA Ops:
  0.0 5.8 %collective-permute-start = (bf16[4,6144]{1,0:T(4,128)(2,1)}, bf16[4,6144]{1,0:T(4,128)(2,1)S(1)}, u32[]{:S(2)}, u32[]{:S(2)}) collective-permute-start(bf16[4,6144]{1,0:T(4,128)(2,1)} %tokens.3), channel_id=1, source_target_pairs={{0,2},{2,0},{1,3},{3,1},{4,6},{6,4},{5,7},{7,5},{8,10},{10,8},{9,1... | collective-permute-start | bytes 147464 | tf_op jit(solution)/shard_map/ppermute | solution.py:30
  3.0 0.8 copy-start.1
  3.9 0.7 copy-start.3
  4.6 33.7 %copy-start.6 = (bf16[768,128]{1,0:T(8,128)(2,1)S(1)}, bf16[768,128]{1,0:T(8,128)(2,1)}, u32[]{:S(2)}) copy-start(bf16[768,128]{1,0:T(8,128)(2,1)} %param.12) | copy-start | bytes 589828
  5.8 32.6 %copy-start.7 = (bf16[768,128]{1,0:T(8,128)(2,1)S(1)}, bf16[768,128]{1,0:T(8,128)(2,1)}, u32[]{:S(2)}) copy-start(bf16[768,128]{1,0:T(8,128)(2,1)} %param.13) | copy-start | bytes 589828
  7.0 31.4 %copy-start.8 = (bf16[768,128]{1,0:T(8,128)(2,1)S(1)}, bf16[768,128]{1,0:T(8,128)(2,1)}, u32[]{:S(2)}) copy-start(bf16[768,128]{1,0:T(8,128)(2,1)} %param.14) | copy-start | bytes 589828
  7.0 33.9 %copy-start.5 = (bf16[768,768]{1,0:T(8,128)(2,1)S(1)}, bf16[768,768]{1,0:T(8,128)(2,1)}, u32[]{:S(2)}) copy-start(bf16[768,768]{1,0:T(8,128)(2,1)} %param.18) | copy-start | bytes 3538948
  7.0 31.3 %all-to-all-start = ((bf16[32,8,1536]{2,1,0:T(8,128)(2,1)}), bf16[32,8,1536]{2,1,0:T(8,128)(2,1)S(1)}, u32[]{:S(2)}, u32[]{:S(2)}) async-start(bf16[32,8,1536]{2,1,0:T(8,128)(2,1)} %normed_pieces.1), calls=%async_computation | async-start | bytes 1572864 | tf_op jit(solution)/shard_map/all_to_all | solution.py:34
  18.9 29.2 %collective-permute-start.3 = (bf16[768,768]{1,0:T(8,128)(2,1)}, bf16[768,768]{1,0:T(8,128)(2,1)}, u32[]{:S(2)}, u32[]{:S(2)}) collective-permute-start(bf16[768,768]{1,0:T(8,128)(2,1)} %w_own.3), channel_id=1, source_target_pairs={{0,128},{128,0},{1,129},{129,1},{2,130},{130,2},{3,131},{131,3},{4... | collective-permute-start | bytes 3538952 | tf_op jit(solution)/shard_map/ppermute | solution.py:30
  38.3 12.3 %collective-permute-start.1 = (bf16[4,64,1536]{2,1,0:T(8,128)(2,1)S(1)}, bf16[4,64,1536]{2,1,0:T(8,128)(2,1)S(1)}, u32[]{:S(2)}, u32[]{:S(2)}) collective-permute-start(bf16[4,64,1536]{2,1,0:T(8,128)(2,1)S(1)} %bitcast.2), channel_id=1, source_target_pairs={{0,1},{1,0},{2,3},{3,2},{4,5},{5,4},{6,7},{7,6},{8,9},{9,8},{10,11... | collective-permute-start | bytes 2359304 | tf_op jit(solution)/shard_map/ppermute | solution.py:30
  38.5 22.1 %collective-permute-start.2 = (bf16[768,384]{1,0:T(8,128)(2,1)S(1)}, bf16[768,384]{1,0:T(8,128)(2,1)S(1)}, u32[]{:S(2)}, u32[]{:S(2)}) collective-permute-start(bf16[768,384]{1,0:T(8,128)(2,1)S(1)} %constant_dynamic-update-slice_fusion.w_own), channel_id=1, source_target_pairs={{0,128},{128,0},{1,129},{129,1},{2,130},{130,2},{3,131},{131,3},{4... | collective-permute-start | bytes 1769480 | tf_op jit(solution)/shard_map/ppermute | solution.py:30
  41.1 54.3 %collective-permute-start.4 = (bf16[896,768]{1,0:T(8,128)(2,1)S(1)}, bf16[896,768]{1,0:T(8,128)(2,1)S(1)}, u32[]{:S(2)}, u32[]{:S(2)}) collective-permute-start(bf16[896,768]{1,0:T(8,128)(2,1)S(1)} %constant_dynamic-update-slice_fusion.3.w_own), channel_id=1, source_target_pairs={{0,128},{128,0},{1,129},{129,1},{2,130},{130,2},{3,131},{131,3},{4... | collective-permute-start | bytes 4128776 | tf_op jit(solution)/shard_map/ppermute | solution.py:30
  62.4 1.0 copy-start
  63.4 16.5 %copy-start.4 = (f32[768]{0:T(1024)S(1)}, f32[768]{0:T(1024)}, u32[]{:S(2)}) copy-start(f32[768]{0:T(1024)} %bias.1) | copy-start | bytes 9220
  63.4 16.5 %all-to-all-start.1 = ((bf16[4,128,1152]{2,1,0:T(8,128)(2,1)}), bf16[4,128,1152]{2,1,0:T(8,128)(2,1)}, u32[]{:S(2)}, u32[]{:S(2)}) async-start(bf16[4,128,1152]{2,1,0:T(8,128)(2,1)} %copy-done), calls=%async_computation.1 | async-start | bytes 2359296 | tf_op jit(solution)/shard_map/all_to_all | solution.py:34
  97.2 2.4 %collective-permute-start.5 = (bf16[4,64,1536]{2,1,0:T(8,128)(2,1)S(1)}, bf16[4,64,1536]{2,1,0:T(8,128)(2,1)S(1)}, u32[]{:S(2)}, u32[]{:S(2)}) collective-permute-start(bf16[4,64,1536]{2,1,0:T(8,128)(2,1)S(1)} %output_sent.1), channel_id=1, source_target_pairs={{0,1},{1,0},{2,3},{3,2},{4,5},{5,4},{6,7},{7,6},{8,9},{9,8},{10,11... | collective-permute-start | bytes 2359304 | tf_op jit(solution)/shard_map/ppermute | solution.py:30
  99.7 35.9 %copy-start.2 = (bf16[4,6144]{1,0:T(4,128)(2,1)S(1)}, bf16[4,6144]{1,0:T(4,128)(2,1)}, u32[]{:S(2)}) copy-start(bf16[4,6144]{1,0:T(4,128)(2,1)} %tokens.3) | copy-start | bytes 147460
